TPU v7x, 128 devices: a whole 4x4x4 slice. The times are simulated.
128 devices in a mesh: member: 4 (over z_hi, core), py: 4 (over x), pz: 8 (over y, z_lo).
Axes of the slice: x: 4, y: 4, z: 4 (z_hi: 2, z_lo: 2; z = z_hi * 2 + z_lo), core: 2. Of those that a mesh axis runs over, the one named last changes fastest.
Arguments:
- velocity_hat: float32 [8, 3, 96, 36864], P('member', None, None, ('py', 'pz')), parts along dimension 0, may hold values from -448 to 448
- time_step: float32 [4], P('member'), parts along dimension 0, may hold values from 0.003 to 0.006
- power: float32 [4], P('member'), parts along dimension 0, may hold values from 20 to 80
- cutoffs: int32 [12], P('member'), parts along dimension 0, may hold values from 48 to 64, as said below
Outputs:
- velocity_next: float32 [8, 3, 96, 36864], P('member', None, None, ('py', 'pz')), parts along dimension 0
- cfl_number: float32 [4], P('member'), parts along dimension 0
- energy: float32 [4], P('member'), parts along dimension 0
There are 4 independent parts, one for each index of `member`. A program takes and returns all parts, laid end to end along the dimension named above; each array names one. Nothing has to cross between parts.
Inputs may be any that keep to these rules, and one draw needn't show every extreme that they name: `cutoffs`: in every draw one of the three equals 64.
All inputs are finite; a program needn't handle non-finite values.
Results may differ from a plain program's by a relative error of at most 0.0002.
Values sent between devices are 32-bit elements; how exact they have to be, the bound alone decides.
A program may use at most 128 MiB of HBM per device.

v0:
```python
import functools
import math

import jax
import jax.numpy as jnp
import ml_dtypes
import numpy as np
from jax import lax
from jax.experimental import pallas as pl
from jax.experimental.pallas import tpu as pltpu
from jax.sharding import PartitionSpec as P

GRID = 192
PARTS = 32
BAND = 6
DEPTH = 72
LIVE = tuple(range(11)) + tuple(range(21, 32))
viscosity = 0.004
f32 = jnp.float32
bf16 = jnp.bfloat16


def halves(table):
    high = table.astype(ml_dtypes.bfloat16)
    low = (table - high.astype(np.float64)).astype(ml_dtypes.bfloat16)
    return np.stack([high, low])


def angle(rows, cols):
    turns = np.outer(rows, cols) % GRID
    return turns * (2.0 * math.pi / GRID)


@functools.lru_cache
def tables():
    n = GRID
    every = np.arange(n)
    phase = angle(every, every)
    tx = np.zeros((2, PARTS, 8, 512))
    cosine, sine = (f(phase).reshape(PARTS, BAND, n) for f in (np.cos, np.sin))
    tx[0, :, :BAND, :n], tx[0, :, :BAND, 256 : 256 + n] = cosine, -sine
    tx[1, :, :BAND, :n], tx[1, :, :BAND, 256 : 256 + n] = sine, cosine
    tx = tx.reshape(512, 512)
    ey = np.zeros((2 * n, 2 * n))
    for at, band in enumerate(LIVE):
        phase = angle(every, band * BAND + np.arange(BAND))
        cols = slice(8 * at, 8 * at + BAND)
        ey[:n, cols] = np.cos(phase)
        ey[n:, cols] = np.sin(phase)
        cols = slice(n + 8 * at, n + 8 * at + BAND)
        ey[:n, cols] = -np.sin(phase)
        ey[n:, cols] = np.cos(phase)
    factor = float(n) ** -1.5
    depth = np.arange(n // 3 + 1)
    phase = angle(depth, every)
    weight = np.where(depth == 0, 1.0, 2.0)[:, None] * factor
    zt = np.zeros((256, n))
    zt[: len(depth)] = weight * np.cos(phase)
    zt[128 : 128 + len(depth)] = -weight * np.sin(phase)
    zb = np.zeros((n, 256))
    zb[:, : len(depth)] = factor * np.cos(phase.T)
    zb[:, 128 : 128 + len(depth)] = -factor * np.sin(phase.T)
    eyt = np.zeros((272, 2 * n))
    for at, band in enumerate(LIVE):
        phase = angle(band * BAND + np.arange(BAND), every)
        rows = slice(12 * at, 12 * at + BAND)
        eyt[rows, :n], eyt[rows, n:] = np.cos(phase), np.sin(phase)
        rows = slice(12 * at + BAND, 12 * at + 2 * BAND)
        eyt[rows, :n], eyt[rows, n:] = -np.sin(phase), np.cos(phase)
    return tuple(halves(t) for t in (tx, ey, zt, zb, eyt))


def split(value):
    high = value.astype(bf16)
    return high, (value - high.astype(f32)).astype(bf16)


def table_by_data(table, data, dims):
    high, low = split(data)
    dot = functools.partial(
        lax.dot_general, dimension_numbers=(dims, ((), ())), preferred_element_type=f32
    )
    return dot(table[0], high) + dot(table[0], low) + dot(table[1], high)


def data_by_table(data, table):
    high, low = split(data)
    dot = functools.partial(jnp.dot, preferred_element_type=f32)
    return dot(high, table[0]) + dot(low, table[0]) + dot(high, table[1])


def signed(index):
    return jnp.where(index < GRID // 2, index, index - GRID)


def pair_waves(pair, cut_ref):
    band = lax.axis_index("py") * lax.axis_size("pz") + lax.axis_index("pz")
    lane = lax.broadcasted_iota(jnp.int32, (DEPTH, 384), 1)
    upper = lane >= GRID
    kx = signed(jnp.where(upper, lane - GRID, lane))
    ky = signed(band * BAND + 2 * pair + upper.astype(jnp.int32))
    kz = lax.broadcasted_iota(jnp.int32, (DEPTH, 384), 0)
    keep = (
        (jnp.abs(kx) <= cut_ref[0]) & (jnp.abs(ky) <= cut_ref[1]) & (kz <= cut_ref[2])
    )
    waves = tuple(k.astype(f32) for k in (kx, ky, kz))
    square = waves[0] * waves[0] + waves[1] * waves[1] + waves[2] * waves[2]
    return waves, square, 1.0 / jnp.maximum(square, 1.0), keep


def project(field, waves, inverse, keep):
    normal = (waves[0] * field[0] + waves[1] * field[1] + waves[2] * field[2]) * inverse
    return [jnp.where(keep, field[a] - waves[a] * normal, 0.0) for a in range(3)]


def spread_kernel(cut_ref, in_ref, tx_ref, out_ref, data, made):
    data[5 * DEPTH :, :] = jnp.zeros((384 - 5 * DEPTH, 512), f32)

    def step(pair, carry):
        window = pl.ds(pl.multiple_of(pair * 384, 128), 384)
        waves, _, inverse, keep = pair_waves(pair, cut_ref)
        parts = []
        for c in range(2):
            field = [in_ref[c, a, :, window] for a in range(3)]
            sol = project(field, waves, inverse, keep)
            curl_y = waves[2] * sol[0] - waves[0] * sol[2]
            curl_z = waves[0] * sol[1] - waves[1] * sol[0]
            parts.append((sol, (curl_y, curl_z)))
        fields = (
            parts[0][0] + [-parts[1][1][0], -parts[1][1][1]],
            parts[1][0] + [parts[0][1][0], parts[0][1][1]],
        )
        for odd in range(2):
            for c in range(2):
                for f in range(5):
                    value = fields[c][f]
                    if odd:
                        value = pltpu.roll(value[:, 128:], 192, 1)
                    else:
                        value = value[:, :256]
                    data[f * DEPTH : (f + 1) * DEPTH, c * 256 : (c + 1) * 256] = value
            made[odd] = table_by_data(tx_ref, data[...], ((1,), (1,)))
        rows = pl.ds(pl.multiple_of(pair * 24, 8), 24)
        for d in range(PARTS):
            pieces = [
                made[odd, c * 256 + d * 8 : c * 256 + d * 8 + BAND, :]
                for odd in range(2)
                for c in range(2)
            ]
            piece = jnp.concatenate(pieces, axis=0)
            for third in range(3):
                out_ref[d, third, rows, :] = piece[:, third * 128 : (third + 1) * 128]
        return carry

    lax.fori_loop(0, 3, step, 0)


def grid_kernel(in_ref, ey_ref, zt_ref, zb_ref, eyt_ref, out_ref, rows_ref, strips, physical, back, made, top, total):
    rows_ref[...] = jnp.zeros_like(rows_ref)
    top[...] = jnp.zeros_like(top)
    total[...] = jnp.zeros_like(total)
    at = lax.broadcasted_iota(jnp.int32, (192, DEPTH), 0)
    band = at // 8
    band = jnp.where(band < 11, band, band + 10)
    ky = signed(band * BAND + at % 8).astype(f32)
    kz = lax.broadcasted_iota(jnp.int32, (192, DEPTH), 1).astype(f32)
    lane = lax.broadcasted_iota(jnp.int32, (192, 128), 1)

    def step(pair, carry):
        for odd in range(2):
            x = 2 * pair + odd
            for c in range(2):
                for i, s in enumerate(LIVE):
                    for third in range(3):
                        rows_ref[
                            c * 192 + 8 * i : c * 192 + 8 * i + BAND,
                            third * 128 : (third + 1) * 128,
                        ] = in_ref[s, third, pl.ds(c * BAND + x, BAND, stride=12), :]
            turned = [
                ky * rows_ref[c * 192 : (c + 1) * 192, 144:216]
                - kz * rows_ref[c * 192 : (c + 1) * 192, 72:144]
                for c in range(2)
            ]
            rows_ref[:192, 384 : 384 + DEPTH] = -turned[1]
            rows_ref[192:, 384 : 384 + DEPTH] = turned[0]
            strips[...] = table_by_data(ey_ref, rows_ref[...], ((1,), (0,)))
            for f in range(6):
                low = 72 * f if f < 5 else 384
                both = jnp.concatenate(
                    [strips[:192, low : low + 128], strips[192:, low : low + 128]], axis=1
                )
                physical[f] = data_by_table(both, zt_ref)
            u = [physical[f] for f in range(3)]
            w = [physical[5], physical[3], physical[4]]
            speed = jnp.abs(u[0]) + jnp.abs(u[1]) + jnp.abs(u[2])
            squares = u[0] * u[0] + u[1] * u[1] + u[2] * u[2]
            top[...] = jnp.maximum(top[...], jnp.max(speed.reshape(24, 8, GRID), axis=0))
            total[...] += jnp.sum(squares.reshape(24, 8, GRID), axis=0)
            q = [
                data_by_table(u[1] * w[2] - u[2] * w[1], zb_ref),
                data_by_table(u[2] * w[0] - u[0] * w[2], zb_ref),
                data_by_table(u[0] * w[1] - u[1] * w[0], zb_ref),
            ]
            for c in range(2):
                q0, q1, q2 = (part[:, c * 128 : (c + 1) * 128] for part in q)
                q1 = pltpu.roll(q1, 72, 1)
                back[c * 192 : (c + 1) * 192, :128] = jnp.where(lane < 72, q0, q1)
                back[c * 192 : (c + 1) * 192, 128:] = jnp.where(
                    lane < 16, q1, pltpu.roll(q2, 16, 1)
                )
            made[odd] = table_by_data(eyt_ref, back[...], ((1,), (0,)))
        rows = pl.ds(pl.multiple_of(pair * 24, 8), 24)
        for i, s in enumerate(LIVE):
            piece = jnp.concatenate(
                [made[0, 12 * i : 12 * i + 12, :], made[1, 12 * i : 12 * i + 12, :]], axis=0
            )
            for half in range(2):
                out_ref[s, half, rows, :] = piece[:, half * 128 : (half + 1) * 128]
        return carry

    for d in range(11, 21):
        out_ref[d] = jnp.zeros((2, 72, 128), f32)
    lax.fori_loop(0, 3, step, 0)
    fastest = jnp.max(top[...])
    summed = jnp.sum(total[...])
    spare = lax.broadcasted_iota(jnp.int32, (8, 128), 1)
    for d in range(PARTS):
        tile = out_ref[d, 1, :8, :]
        out_ref[d, 1, :8, :] = jnp.where(
            spare == 112, fastest, jnp.where(spare == 113, summed, tile)
        )


def close_kernel(cut_ref, dt_ref, power_ref, old_ref, in_ref, tx_ref, out_ref, cfl_ref, energy_ref, gathered, terms, spectra):
    gathered[...] = jnp.zeros_like(gathered)
    stats = [in_ref[s, 1, :8, :] for s in range(PARTS)]
    fastest, summed = stats[0], stats[0]
    for s in range(1, PARTS):
        fastest = jnp.maximum(fastest, stats[s])
        summed = summed + stats[s]
    spot = lax.broadcasted_iota(jnp.int32, (8, 128), 1)
    first = lax.broadcasted_iota(jnp.int32, (8, 128), 0) == 0
    fastest = jnp.max(jnp.where((spot == 112) & first, fastest, 0.0))
    summed = jnp.sum(jnp.where((spot == 113) & first, summed, 0.0))
    energy = 0.5 * summed * (1.0 / float(GRID**3))
    dt = dt_ref[0]
    cfl_ref[0] = dt * fastest * GRID * (1.0 / (2.0 * math.pi))
    energy_ref[0] = energy
    twice = jnp.maximum(jnp.full((DEPTH, 384), 2.0 * energy, f32), 0.5)
    forcing = power_ref[0] / twice

    out_ref[:, :, DEPTH:, :] = jnp.zeros((2, 3, 96 - DEPTH, 1152), f32)

    def step(pair, carry):
        window = pl.ds(pl.multiple_of(pair * 384, 128), 384)
        for odd in range(2):
            ky = 2 * pair + odd
            for c in range(2):
                for half in range(2):
                    for s in range(PARTS):
                        gathered[8 * s : 8 * s + BAND, :] = in_ref[
                            s, half, pl.ds(c * BAND + ky, BAND, stride=12), :
                        ]
                    terms[half * 128 : (half + 1) * 128, c * 256 : (c + 1) * 256] = gathered[...].T
            spectra[odd] = data_by_table(terms[: 3 * DEPTH, :], tx_ref)
        waves, square, inverse, keep = pair_waves(pair, cut_ref)
        for c in range(2):
            old = project([old_ref[c, a, :, window] for a in range(3)], waves, inverse, keep)
            new = []
            for a in range(3):
                rows = slice(a * DEPTH, (a + 1) * DEPTH)
                even = spectra[0, rows, c * 256 : (c + 1) * 256]
                odd = pltpu.roll(spectra[1, rows, c * 256 : (c + 1) * 256], 64, 1)
                new.append(
                    jnp.concatenate([even[:, :128], even[:, 128:] + odd[:, :128], odd[:, 128:]], axis=1)
                )
            forced = project(new, waves, inverse, keep)
            for a in range(3):
                out_ref[c, a, :DEPTH, window] = old[a] + dt * (
                    forced[a] + forcing * old[a] - viscosity * square * old[a]
                )
        return carry

    lax.fori_loop(0, 3, step, 0)


VM = pl.BlockSpec(memory_space=pltpu.VMEM)
SM = pl.BlockSpec(memory_space=pltpu.SMEM)
GRANT = pltpu.CompilerParams(vmem_limit_bytes=60 * 1024 * 1024)


def on_device(velocity_hat, time_step, power, cutoffs):
    tx, ey, zt, zb, eyt = (jnp.asarray(t) for t in tables())
    shape = jax.ShapeDtypeStruct
    block = pl.BlockSpec((2, 3, DEPTH, 1152), lambda i: (0, 0, 0, 0))
    whole = lambda a: pl.BlockSpec(a.shape, lambda i: (0,) * a.ndim)
    chunks = pl.pallas_call(
        spread_kernel,
        grid=(1,),
        out_shape=shape((PARTS, 3, 72, 128), f32),
        in_specs=[SM, block, whole(tx)],
        out_specs=pl.BlockSpec((PARTS, 3, 72, 128), lambda i: (0, 0, 0, 0)),
        scratch_shapes=[pltpu.VMEM((384, 512), f32), pltpu.VMEM((2, 512, 384), f32)],
        compiler_params=GRANT,
    )(cutoffs, velocity_hat, tx)
    chunks = lax.all_to_all(chunks, ("py", "pz"), 0, 0, tiled=True)
    chunks = pl.pallas_call(
        grid_kernel,
        out_shape=shape((PARTS, 2, 72, 128), f32),
        in_specs=[VM] * 5,
        out_specs=VM,
        scratch_shapes=[
            pltpu.VMEM((384, 512), f32),
            pltpu.VMEM((384, 512), f32),
            pltpu.VMEM((6, GRID, GRID), f32),
            pltpu.VMEM((384, 256), f32),
            pltpu.VMEM((2, 272, 256), f32),
            pltpu.VMEM((8, GRID), f32),
            pltpu.VMEM((8, GRID), f32),
        ],
        compiler_params=GRANT,
    )(chunks, ey, zt, zb, eyt)
    chunks = lax.all_to_all(chunks, ("py", "pz"), 0, 0, tiled=True)
    return pl.pallas_call(
        close_kernel,
        grid=(1,),
        out_shape=(shape((2, 3, 96, 1152), f32), shape((1,), f32), shape((1,), f32)),
        in_specs=[SM, SM, SM, block, whole(chunks), whole(tx)],
        out_specs=(pl.BlockSpec((2, 3, 96, 1152), lambda i: (0, 0, 0, 0)), SM, SM),
        scratch_shapes=[pltpu.VMEM((256, 128), f32), pltpu.VMEM((256, 512), f32), pltpu.VMEM((2, 3 * DEPTH, 512), f32)],
        compiler_params=GRANT,
    )(cutoffs, time_step, power, velocity_hat, chunks, tx)


def solution(mesh):
    return jax.shard_map(
        on_device,
        mesh=mesh,
        in_specs=(P("member", None, None, ("py", "pz")), P("member"), P("member"), P("member")),
        out_specs=(P("member", None, None, ("py", "pz")), P("member"), P("member")),
        check_vma=False,
    )
```

profile of v0, /device:TPU:0, one launch (start us, length us, event | category | flops | bytes accessed | tf_op | source)
XLA Modules:
  0.0 128.5 jit_solution(17756147091669961590)
XLA Ops:
  0.6 9.7 %shard_map.112 = f32[32,3,72,128]{3,2,1,0:T(8,128)} custom-call(s32[3]{0:T(128)} %cut_ref.3, f32[2,3,96,1152]{3,2,1,0:T(8,128)} %old_ref.1, bf16[2,512,512]{2,1,0:T(8,128)(2,1)} %constant.10.clone.tx_ref), custom_call_target="tpu_custom_call" | custom-call | tf_op jit(solution)/shard_map/pallas_call | solution.py:297
  10.4 53.0 %all_to_all.10.in_ref = f32[32,3,72,128]{3,2,1,0:T(8,128)} all-to-all(f32[32,3,72,128]{3,2,1,0:T(8,128)} %shard_map.112), channel_id=1, replica_groups=mesh['member'=4,'py'=4,'pz'=8] {'py','pz'}, dimensions={0} | all-to-all | bytes 7077888 | tf_op jit(solution)/shard_map/all_to_all | solution.py:306
  63.4 19.9 %shard_map.113 = f32[32,2,72,128]{3,2,1,0:T(8,128)} custom-call(f32[32,3,72,128]{3,2,1,0:T(8,128)} %all_to_all.10.in_ref, bf16[2,384,384]{2,1,0:T(8,128)(2,1)} %constant.11.clone.ey_ref, bf16[2,256,192]{2,1,0:T(8,128)(2,1)} %constant.12.clone.zt_ref, bf16[2,192,256]{2,1,0:T(8,128)(2,1)} %constant.13.clone.zb_ref, bf16[2,272,384]{2,1,0:T(8,128)(2,1)} %constant.14.clone.eyt_ref), custom_call_target="tpu_custom_call" | custom-call | tf_op jit(solution)/shard_map/pallas_call | solution.py:307
  83.3 4.1 %all-to-all-start.1 = ((f32[32,2,72,128]{3,2,1,0:T(8,128)}), f32[32,2,72,128]{3,2,1,0:T(8,128)S(1)}, u32[]{:S(2)}, u32[]{:S(2)}) async-start(f32[32,2,72,128]{3,2,1,0:T(8,128)} %shard_map.113), calls=%async_computation.1 | async-start | bytes 4718592 | tf_op jit(solution)/shard_map/all_to_all | solution.py:323
  88.7 30.0 %all-to-all-done.1.in_ref = f32[32,2,72,128]{3,2,1,0:T(8,128)S(1)} async-done(((f32[32,2,72,128]{3,2,1,0:T(8,128)}), f32[32,2,72,128]{3,2,1,0:T(8,128)S(1)}, u32[]{:S(2)}, u32[]{:S(2)}) %all-to-all-start.1) | async-done | bytes 2359328 | tf_op jit(solution)/shard_map/all_to_all | solution.py:323
  118.7 0.0 copy-start
  118.7 1.4 %copy-done = f32[32,2,72,128]{3,2,1,0:T(8,128)} copy-done((f32[32,2,72,128]{3,2,1,0:T(8,128)}, f32[32,2,72,128]{3,2,1,0:T(8,128)S(1)}, u32[]{:S(2)}) %copy-start) | copy-done | bytes 2359320
  120.1 8.3 %shard_map.114 = (f32[2,3,96,1152]{3,2,1,0:T(8,128)}, f32[1]{0:T(128)}, f32[1]{0:T(128)}) custom-call(s32[3]{0:T(128)} %cut_ref.3, f32[1]{0:T(128)S(6)} %copy.12.dt_ref, f32[1]{0:T(128)S(6)} %copy.13.power_ref, f32[2,3,96,1152]{3,2,1,0:T(8,128)} %old_ref.1, f32[32,2,72,128]{3,2,1,0:T(8,128)} %copy-done, bf16[2,512,512]{2,1,0:T(8,128)(2,1)} %constant.10.clone.tx_ref), custom_call_target="tpu_custom_call" | custom-call | tf_op jit(solution)/shard_map/pallas_call | solution.py:324
Async XLA Ops:
  83.3 35.5 %all-to-all-start.1 = ((f32[32,2,72,128]{3,2,1,0:T(8,128)}), f32[32,2,72,128]{3,2,1,0:T(8,128)S(1)}, u32[]{:S(2)}, u32[]{:S(2)}) async-start(f32[32,2,72,128]{3,2,1,0:T(8,128)} %shard_map.113), calls=%async_computation.1 | async-start | bytes 4718592 | tf_op jit(solution)/shard_map/all_to_all | solution.py:323
  118.7 1.4 %copy-start = (f32[32,2,72,128]{3,2,1,0:T(8,128)}, f32[32,2,72,128]{3,2,1,0:T(8,128)S(1)}, u32[]{:S(2)}) copy-start(f32[32,2,72,128]{3,2,1,0:T(8,128)S(1)} %all-to-all-done.1.in_ref) | copy-start | bytes 7077892
where the time goes:
time: 129 us; the launch traced here: 128 us
  blocking collectives  53 us (41%)
  Pallas kernels  37.9 us (29%)
  waiting for transfers between devices  30 us (23%)
  starting transfers between devices  4.14 us (3%)
  between operations  1.93 us (1%)
  local copies, waits for them, and re-layouts  1.42 us (1%)
    all_to_all x1, blocking collectives, on_device(): chunks = lax.all_to_all(chunks, ('py', 'pz'), 0, 0, tiled=True)  53 us
    all_to_all x1, waiting for transfers between devices, on_device(): chunks = lax.all_to_all(chunks, ('py', 'pz'), 0, 0, tiled=True)  30 us
    pallas_call x1, Pallas kernels, on_device(): pl.pallas_call(grid_kernel, out_shape=shape((PARTS, 2, 72, 128), f32), in...  19.9 us
    pallas_call x1, Pallas kernels, on_device(): pl.pallas_call(spread_kernel, grid=(1,), out_shape=shape((PARTS, 3, 72, 1...  9.73 us
    pallas_call x1, Pallas kernels, on_device(): pl.pallas_call(close_kernel, grid=(1,), out_shape=(shape((2, 3, 96, 1152)...  8.34 us
    all_to_all x1, starting transfers between devices, on_device(): chunks = lax.all_to_all(chunks, ('py', 'pz'), 0, 0, tiled=True)  4.14 us
  transfers between devices with their start and end apart: 1, of which 1 were waited for; matrix products, arithmetic and copies ran while one was open for 0% of the time, Pallas kernels for 0%

commit v1 on v0

--- a/solution.py
+++ b/solution.py
@@ -113,49 +113,123 @@
     return [jnp.where(keep, field[a] - waves[a] * normal, 0.0) for a in range(3)]
 
 
-def spread_kernel(cut_ref, in_ref, tx_ref, out_ref, data, made):
+MESH = pl.DeviceIdType.MESH
+TURNS = ((1, 1), (3, 0), (2, 1), (0, 0), (1, 0), (3, 1), (2, 0), (0, 1))
+OFFSETS = tuple(
+    (dx, *TURNS[(k + 2 * j) % 8]) for k in range(8) for j, dx in enumerate((2, 1, 3, 0))
+)
+
+
+def is_live(band):
+    return (band < 11) | (band >= 21)
+
+
+def exchange_kernel(
+    cut_ref, in_hbm, tx_hbm, ey_hbm, zt_hbm, zb_hbm, eyt_hbm, out_hbm, stats_hbm,
+    held, tx_ref, ey_ref, zt_ref, zb_ref, eyt_ref, data, made, ready, arrived,
+    rows_ref, strips, physical, back, closed, answer, top, total, stat,
+    load_sems, send_sems, recv_sems, back_send, back_recv, stat_send, stat_recv, own_sems,
+):
+    px, pz = lax.axis_index("py"), lax.axis_index("pz")
+    me = px * 8 + pz
+
+    def peer(offset):
+        x = lax.rem(px + offset[0], 4)
+        y = lax.rem(pz // 2 + offset[1], 4)
+        z = lax.rem(pz % 2 + offset[2], 2)
+        return x, y * 2 + z
+
+    def flat(device):
+        return device[0] * 8 + device[1]
+
+    def to(device):
+        return {"py": device[0], "pz": device[1]}
+
+    others = [(j, offset) for j, offset in enumerate(OFFSETS) if offset != (0, 0, 0)]
+    self_slot = OFFSETS.index((0, 0, 0))
+
+    loads = [
+        pltpu.make_async_copy(
+            in_hbm.at[:, :, pl.ds(0, DEPTH), pl.ds(384 * p, 384)], held.at[p], load_sems.at[p]
+        )
+        for p in range(3)
+    ]
+    tabled = [
+        pltpu.make_async_copy(source, target, load_sems.at[3 + k])
+        for k, (source, target) in enumerate(
+            ((tx_hbm, tx_ref), (ey_hbm, ey_ref), (zt_hbm, zt_ref), (zb_hbm, zb_ref), (eyt_hbm, eyt_ref))
+        )
+    ]
+    for copy in (loads[0], tabled[0], *loads[1:], *tabled[1:]):
+        copy.start()
+
+    barrier = pltpu.get_barrier_semaphore()
+    for _, offset in others:
+        pl.semaphore_signal(barrier, inc=1, device_id=to(peer(offset)), device_id_type=MESH)
+
+    def first_copy(j, device, pair):
+        rows = pl.ds(24 * pair, 24)
+        return pltpu.make_async_remote_copy(
+            src_ref=ready.at[j, :, rows, :],
+            dst_ref=arrived.at[me, :, rows, :],
+            send_sem=send_sems.at[j],
+            recv_sem=recv_sems.at[me],
+            device_id=to(device),
+            device_id_type=MESH,
+        )
+
     data[5 * DEPTH :, :] = jnp.zeros((384 - 5 * DEPTH, 512), f32)
-
-    def step(pair, carry):
-        window = pl.ds(pl.multiple_of(pair * 384, 128), 384)
-        waves, _, inverse, keep = pair_waves(pair, cut_ref)
-        parts = []
-        for c in range(2):
-            field = [in_ref[c, a, :, window] for a in range(3)]
-            sol = project(field, waves, inverse, keep)
-            curl_y = waves[2] * sol[0] - waves[0] * sol[2]
-            curl_z = waves[0] * sol[1] - waves[1] * sol[0]
-            parts.append((sol, (curl_y, curl_z)))
-        fields = (
-            parts[0][0] + [-parts[1][1][0], -parts[1][1][1]],
-            parts[1][0] + [parts[0][1][0], parts[0][1][1]],
-        )
-        for odd in range(2):
+    tabled[0].wait()
+
+    for pair in range(3):
+        loads[pair].wait()
+
+        @pl.when(is_live(me))
+        def _():
+            waves, _, inverse, keep = pair_waves(pair, cut_ref)
+            parts = []
             for c in range(2):
-                for f in range(5):
-                    value = fields[c][f]
-                    if odd:
-                        value = pltpu.roll(value[:, 128:], 192, 1)
+                sol = project([held[pair, c, a] for a in range(3)], waves, inverse, keep)
+                curl_y = waves[2] * sol[0] - waves[0] * sol[2]
+                curl_z = waves[0] * sol[1] - waves[1] * sol[0]
+                parts.append((sol, (curl_y, curl_z)))
+            fields = (
+                parts[0][0] + [-parts[1][1][0], -parts[1][1][1]],
+                parts[1][0] + [parts[0][1][0], parts[0][1][1]],
+            )
+            for odd in range(2):
+                for c in range(2):
+                    for f in range(5):
+                        value = fields[c][f]
+                        if odd:
+                            value = pltpu.roll(value[:, 128:], 192, 1)
+                        else:
+                            value = value[:, :256]
+                        data[f * DEPTH : (f + 1) * DEPTH, c * 256 : (c + 1) * 256] = value
+                made[odd] = table_by_data(tx_ref, data[...], ((1,), (1,)))
+
+        if pair == 0:
+            pl.semaphore_wait(barrier, PARTS - 1)
+
+        @pl.when(is_live(me))
+        def _():
+            for j, offset in enumerate(OFFSETS):
+                d = flat(peer(offset))
+                pieces = [
+                    made[odd, pl.ds(pl.multiple_of(c * 256 + d * 8, 8), 8), :][:BAND]
+                    for odd in range(2)
+                    for c in range(2)
+                ]
+                piece = jnp.concatenate(pieces, axis=0)
+                for third in range(3):
+                    part = piece[:, third * 128 : (third + 1) * 128]
+                    if j == self_slot:
+                        arrived[me, third, 24 * pair : 24 * pair + 24, :] = part
                     else:
-                        value = value[:, :256]
-                    data[f * DEPTH : (f + 1) * DEPTH, c * 256 : (c + 1) * 256] = value
-            made[odd] = table_by_data(tx_ref, data[...], ((1,), (1,)))
-        rows = pl.ds(pl.multiple_of(pair * 24, 8), 24)
-        for d in range(PARTS):
-            pieces = [
-                made[odd, c * 256 + d * 8 : c * 256 + d * 8 + BAND, :]
-                for odd in range(2)
-                for c in range(2)
-            ]
-            piece = jnp.concatenate(pieces, axis=0)
-            for third in range(3):
-                out_ref[d, third, rows, :] = piece[:, third * 128 : (third + 1) * 128]
-        return carry
-
-    lax.fori_loop(0, 3, step, 0)
-
-
-def grid_kernel(in_ref, ey_ref, zt_ref, zb_ref, eyt_ref, out_ref, rows_ref, strips, physical, back, made, top, total):
+                        ready[j, third, 24 * pair : 24 * pair + 24, :] = part
+                if j != self_slot:
+                    first_copy(j, peer(offset), pair).start()
+
     rows_ref[...] = jnp.zeros_like(rows_ref)
     top[...] = jnp.zeros_like(top)
     total[...] = jnp.zeros_like(total)
@@ -165,9 +239,39 @@
     ky = signed(band * BAND + at % 8).astype(f32)
     kz = lax.broadcasted_iota(jnp.int32, (192, DEPTH), 1).astype(f32)
     lane = lax.broadcasted_iota(jnp.int32, (192, 128), 1)
-
-    def step(pair, carry):
-        for odd in range(2):
+    for copy in tabled[1:]:
+        copy.wait()
+
+    def whole_first(slot, source):
+        return pltpu.make_async_remote_copy(
+            src_ref=ready.at[slot],
+            dst_ref=arrived.at[source],
+            send_sem=send_sems.at[slot],
+            recv_sem=recv_sems.at[source],
+            device_id=to((px, pz)),
+            device_id_type=MESH,
+        )
+
+    for s in LIVE:
+
+        @pl.when(s != me)
+        def _():
+            whole_first(0, s).wait_recv()
+
+    def second_copy(j, device, pair):
+        rows = pl.ds(24 * pair, 24)
+        return pltpu.make_async_remote_copy(
+            src_ref=answer.at[flat(device), :, rows, :],
+            dst_ref=out_hbm.at[me, :, rows, :],
+            send_sem=back_send.at[j],
+            recv_sem=back_recv.at[me],
+            device_id=to(device),
+            device_id_type=MESH,
+        )
+
+    for pair in range(3):
+
+        def one(odd, carry):
             x = 2 * pair + odd
             for c in range(2):
                 for i, s in enumerate(LIVE):
@@ -175,7 +279,7 @@
                         rows_ref[
                             c * 192 + 8 * i : c * 192 + 8 * i + BAND,
                             third * 128 : (third + 1) * 128,
-                        ] = in_ref[s, third, pl.ds(c * BAND + x, BAND, stride=12), :]
+                        ] = arrived[s, third, pl.ds(c * BAND + x, BAND, stride=12), :]
             turned = [
                 ky * rows_ref[c * 192 : (c + 1) * 192, 144:216]
                 - kz * rows_ref[c * 192 : (c + 1) * 192, 72:144]
@@ -208,40 +312,90 @@
                 back[c * 192 : (c + 1) * 192, 128:] = jnp.where(
                     lane < 16, q1, pltpu.roll(q2, 16, 1)
                 )
-            made[odd] = table_by_data(eyt_ref, back[...], ((1,), (0,)))
-        rows = pl.ds(pl.multiple_of(pair * 24, 8), 24)
+            closed[odd] = table_by_data(eyt_ref, back[...], ((1,), (0,)))
+            return carry
+
+        lax.fori_loop(0, 2, one, 0)
         for i, s in enumerate(LIVE):
             piece = jnp.concatenate(
-                [made[0, 12 * i : 12 * i + 12, :], made[1, 12 * i : 12 * i + 12, :]], axis=0
+                [closed[0, 12 * i : 12 * i + 12, :], closed[1, 12 * i : 12 * i + 12, :]], axis=0
             )
             for half in range(2):
-                out_ref[s, half, rows, :] = piece[:, half * 128 : (half + 1) * 128]
-        return carry
-
-    for d in range(11, 21):
-        out_ref[d] = jnp.zeros((2, 72, 128), f32)
-    lax.fori_loop(0, 3, step, 0)
-    fastest = jnp.max(top[...])
-    summed = jnp.sum(total[...])
-    spare = lax.broadcasted_iota(jnp.int32, (8, 128), 1)
-    for d in range(PARTS):
-        tile = out_ref[d, 1, :8, :]
-        out_ref[d, 1, :8, :] = jnp.where(
-            spare == 112, fastest, jnp.where(spare == 113, summed, tile)
-        )
-
-
-def close_kernel(cut_ref, dt_ref, power_ref, old_ref, in_ref, tx_ref, out_ref, cfl_ref, energy_ref, gathered, terms, spectra):
+                answer[s, half, 24 * pair : 24 * pair + 24, :] = piece[
+                    :, half * 128 : (half + 1) * 128
+                ]
+        for j, offset in others:
+            device = peer(offset)
+
+            @pl.when(is_live(flat(device)))
+            def _():
+                second_copy(j, device, pair).start()
+
+    spot = lax.broadcasted_iota(jnp.int32, (8, 128), 1)
+    stat[...] = jnp.where(spot == 0, jnp.max(top[...]), jnp.sum(total[...]))
+
+    def stat_copy(j, device):
+        return pltpu.make_async_remote_copy(
+            src_ref=stat,
+            dst_ref=stats_hbm.at[me],
+            send_sem=stat_send.at[j],
+            recv_sem=stat_recv.at[me],
+            device_id=to(device),
+            device_id_type=MESH,
+        )
+
+    own = (
+        pltpu.make_async_copy(answer.at[me], out_hbm.at[me], own_sems.at[0]),
+        pltpu.make_async_copy(stat, stats_hbm.at[me], own_sems.at[1]),
+    )
+    pl.when(is_live(me))(own[0].start)
+    own[1].start()
+    for j, offset in others:
+        stat_copy(j, peer(offset)).start()
+    pl.when(is_live(me))(own[0].wait)
+    own[1].wait()
+
+    def whole_second(j, source):
+        return pltpu.make_async_remote_copy(
+            src_ref=answer.at[0],
+            dst_ref=out_hbm.at[source],
+            send_sem=back_send.at[j],
+            recv_sem=back_recv.at[source],
+            device_id=to((px, pz)),
+            device_id_type=MESH,
+        )
+
+    for j, offset in others:
+        device = peer(offset)
+        stat_copy(j, device).wait_send()
+        pl.when(is_live(me))(whole_first(j, 0).wait_send)
+        pl.when(is_live(flat(device)))(whole_second(j, 0).wait_send)
+    for s in range(PARTS):
+
+        @pl.when(s != me)
+        def _():
+            pltpu.make_async_remote_copy(
+                src_ref=stat,
+                dst_ref=stats_hbm.at[s],
+                send_sem=stat_send.at[0],
+                recv_sem=stat_recv.at[s],
+                device_id=to((px, pz)),
+                device_id_type=MESH,
+            ).wait_recv()
+
+        @pl.when((s != me) & is_live(me))
+        def _():
+            whole_second(0, s).wait_recv()
+
+
+def close_kernel(cut_ref, dt_ref, power_ref, old_ref, in_ref, stats_ref, tx_ref, out_ref, cfl_ref, energy_ref, gathered, terms, spectra):
     gathered[...] = jnp.zeros_like(gathered)
-    stats = [in_ref[s, 1, :8, :] for s in range(PARTS)]
-    fastest, summed = stats[0], stats[0]
+    fastest = stats_ref[0]
+    summed = stats_ref[0]
     for s in range(1, PARTS):
-        fastest = jnp.maximum(fastest, stats[s])
-        summed = summed + stats[s]
-    spot = lax.broadcasted_iota(jnp.int32, (8, 128), 1)
-    first = lax.broadcasted_iota(jnp.int32, (8, 128), 0) == 0
-    fastest = jnp.max(jnp.where((spot == 112) & first, fastest, 0.0))
-    summed = jnp.sum(jnp.where((spot == 113) & first, summed, 0.0))
+        fastest = jnp.maximum(fastest, stats_ref[s])
+        summed = summed + stats_ref[s]
+    fastest, summed = jnp.max(fastest[:, :1]), jnp.max(summed[:, 1:2])
     energy = 0.5 * summed * (1.0 / float(GRID**3))
     dt = dt_ref[0]
     cfl_ref[0] = dt * fastest * GRID * (1.0 / (2.0 * math.pi))
@@ -281,12 +435,20 @@
                 )
         return carry
 
-    lax.fori_loop(0, 3, step, 0)
-
-
-VM = pl.BlockSpec(memory_space=pltpu.VMEM)
+    live = is_live(lax.axis_index("py") * lax.axis_size("pz") + lax.axis_index("pz"))
+
+    @pl.when(live)
+    def _():
+        lax.fori_loop(0, 3, step, 0)
+
+    @pl.when(jnp.logical_not(live))
+    def _():
+        out_ref[:, :, :DEPTH, :] = jnp.zeros((2, 3, DEPTH, 1152), f32)
+
+
 SM = pl.BlockSpec(memory_space=pltpu.SMEM)
-GRANT = pltpu.CompilerParams(vmem_limit_bytes=60 * 1024 * 1024)
+ANY = pl.BlockSpec(memory_space=pl.ANY)
+VMEM_BYTES = 60 * 1024 * 1024
 
 
 def on_device(velocity_hat, time_step, power, cutoffs):
@@ -294,42 +456,49 @@
     shape = jax.ShapeDtypeStruct
     block = pl.BlockSpec((2, 3, DEPTH, 1152), lambda i: (0, 0, 0, 0))
     whole = lambda a: pl.BlockSpec(a.shape, lambda i: (0,) * a.ndim)
-    chunks = pl.pallas_call(
-        spread_kernel,
-        grid=(1,),
-        out_shape=shape((PARTS, 3, 72, 128), f32),
-        in_specs=[SM, block, whole(tx)],
-        out_specs=pl.BlockSpec((PARTS, 3, 72, 128), lambda i: (0, 0, 0, 0)),
-        scratch_shapes=[pltpu.VMEM((384, 512), f32), pltpu.VMEM((2, 512, 384), f32)],
-        compiler_params=GRANT,
-    )(cutoffs, velocity_hat, tx)
-    chunks = lax.all_to_all(chunks, ("py", "pz"), 0, 0, tiled=True)
-    chunks = pl.pallas_call(
-        grid_kernel,
-        out_shape=shape((PARTS, 2, 72, 128), f32),
-        in_specs=[VM] * 5,
-        out_specs=VM,
+    dma = pltpu.SemaphoreType.DMA
+    chunks, stats = pl.pallas_call(
+        exchange_kernel,
+        out_shape=(shape((PARTS, 2, 72, 128), f32), shape((PARTS, 8, 128), f32)),
+        in_specs=[SM] + [ANY] * 6,
+        out_specs=(ANY, ANY),
         scratch_shapes=[
+            pltpu.VMEM((3, 2, 3, DEPTH, 384), f32),
+            *(pltpu.VMEM(t.shape, bf16) for t in (tx, ey, zt, zb, eyt)),
+            pltpu.VMEM((384, 512), f32),
+            pltpu.VMEM((2, 512, 384), f32),
+            pltpu.VMEM((PARTS, 3, 72, 128), f32),
+            pltpu.VMEM((PARTS, 3, 72, 128), f32),
             pltpu.VMEM((384, 512), f32),
             pltpu.VMEM((384, 512), f32),
             pltpu.VMEM((6, GRID, GRID), f32),
             pltpu.VMEM((384, 256), f32),
             pltpu.VMEM((2, 272, 256), f32),
+            pltpu.VMEM((PARTS, 2, 72, 128), f32),
             pltpu.VMEM((8, GRID), f32),
             pltpu.VMEM((8, GRID), f32),
+            pltpu.VMEM((8, 128), f32),
+            dma((8,)),
+            *[dma((PARTS,))] * 6,
+            dma((2,)),
         ],
-        compiler_params=GRANT,
-    )(chunks, ey, zt, zb, eyt)
-    chunks = lax.all_to_all(chunks, ("py", "pz"), 0, 0, tiled=True)
+        compiler_params=pltpu.CompilerParams(
+            collective_id=0, has_side_effects=True, vmem_limit_bytes=VMEM_BYTES
+        ),
+    )(cutoffs, velocity_hat, tx, ey, zt, zb, eyt)
     return pl.pallas_call(
         close_kernel,
         grid=(1,),
         out_shape=(shape((2, 3, 96, 1152), f32), shape((1,), f32), shape((1,), f32)),
-        in_specs=[SM, SM, SM, block, whole(chunks), whole(tx)],
+        in_specs=[SM, SM, SM, block, whole(chunks), whole(stats), whole(tx)],
         out_specs=(pl.BlockSpec((2, 3, 96, 1152), lambda i: (0, 0, 0, 0)), SM, SM),
-        scratch_shapes=[pltpu.VMEM((256, 128), f32), pltpu.VMEM((256, 512), f32), pltpu.VMEM((2, 3 * DEPTH, 512), f32)],
-        compiler_params=GRANT,
-    )(cutoffs, time_step, power, velocity_hat, chunks, tx)
+        scratch_shapes=[
+            pltpu.VMEM((256, 128), f32),
+            pltpu.VMEM((256, 512), f32),
+            pltpu.VMEM((2, 3 * DEPTH, 512), f32),
+        ],
+        compiler_params=pltpu.CompilerParams(vmem_limit_bytes=VMEM_BYTES),
+    )(cutoffs, time_step, power, velocity_hat, chunks, stats, tx)
 
 
 def solution(mesh):

time: 129 us -> 96.1 us (0.74)
  Pallas kernels: 37.9 us -> 93.9 us
  blocking collectives: 53 us -> 0 us
  waiting for transfers between devices: 30 us -> 0 us
  starting transfers between devices: 4.14 us -> 0 us
  local copies, waits for them, and re-layouts: 1.42 us -> 0 us
    pallas_call x2 -> x1, Pallas kernels: 29.6 us -> 85.5 us  [on_device(): pl.pallas_call(exchange_kernel, out_shape=(shape((PARTS, 2, 72, 128), f32...]
    all_to_all x1 -> x0, blocking collectives: 53 us -> none  [on_device(): chunks = lax.all_to_all(chunks, ('py', 'pz'), 0, 0, tiled=True)]
    all_to_all x1 -> x0, waiting for transfers between devices: 30 us -> none  [on_device(): chunks = lax.all_to_all(chunks, ('py', 'pz'), 0, 0, tiled=True)]
    all_to_all x1 -> x0, starting transfers between devices: 4.14 us -> none  [on_device(): chunks = lax.all_to_all(chunks, ('py', 'pz'), 0, 0, tiled=True)]
    unnamed x2 -> x0, local copies, waits for them, and re-layouts: 1.42 us -> none
  transfers between devices with their start and end apart: 1 -> 0, of which waited for: 1 -> 0; matrix products, arithmetic and copies ran while one was open for 0% -> 0% of each run, Pallas kernels for 0% -> 0%
where the time goes in v1:
time: 96.1 us; the launch traced here: 96 us
  Pallas kernels  93.9 us (98%)
  between operations  2.09 us (2%)
    pallas_call x1, Pallas kernels, on_device(): pl.pallas_call(exchange_kernel, out_shape=(shape((PARTS, 2, 72, 128), f32...  85.5 us
    pallas_call x1, Pallas kernels, on_device(): pl.pallas_call(close_kernel, grid=(1,), out_shape=(shape((2, 3, 96, 1152)...  8.4 us

profile of v1, /device:TPU:0, one launch (start us, length us, event | category | flops | bytes accessed | tf_op | source)
XLA Modules:
  0.0 96.0 jit_solution(14962279210158794961)
XLA Ops:
  1.9 85.5 %shard_map.112 = (f32[32,2,72,128]{3,2,1,0:T(8,128)}, f32[32,8,128]{2,1,0:T(8,128)}) custom-call(s32[3]{0:T(128)} %cut_ref.3, f32[2,3,96,1152]{3,2,1,0:T(8,128)} %old_ref.1, bf16[2,512,512]{2,1,0:T(8,128)(2,1)} %constant.10.clone.tx_hbm.tx_ref, bf16[2,384,384]{2,1,0:T(8,128)(2,1)} %constant.11.clone.ey_hbm, bf16[2,256,192]{2,1,0:T(8,128)(2,1)} %constant.12.clone.zt_hbm, ...), custom_call_target="tpu_custom_call" | custom-call | tf_op jit(solution)/shard_map/pallas_call | solution.py:460
  87.4 8.4 %shard_map.113 = (f32[2,3,96,1152]{3,2,1,0:T(8,128)}, f32[1]{0:T(128)}, f32[1]{0:T(128)}) custom-call(s32[3]{0:T(128)} %cut_ref.3, f32[1]{0:T(128)S(6)} %copy.12.dt_ref, f32[1]{0:T(128)S(6)} %copy.13.power_ref, f32[2,3,96,1152]{3,2,1,0:T(8,128)} %old_ref.1, f32[32,2,72,128]{3,2,1,0:T(8,128)} %get-tuple-element.5.in_ref, ...), custom_call_target="tpu_custom_call" | custom-call | tf_op jit(solution)/shard_map/pallas_call | solution.py:489

commit v2 on v1

v2 whole, which is shorter than its diff:
```python
import functools
import math

import jax
import jax.numpy as jnp
import ml_dtypes
import numpy as np
from jax import lax
from jax.experimental import pallas as pl
from jax.experimental.pallas import tpu as pltpu
from jax.sharding import PartitionSpec as P

GRID = 192
PARTS = 32
BAND = 6
DEPTH = 72
LIVE = tuple(range(11)) + tuple(range(21, 32))
viscosity = 0.004
f32 = jnp.float32
bf16 = jnp.bfloat16


def halves(table):
    high = table.astype(ml_dtypes.bfloat16)
    low = (table - high.astype(np.float64)).astype(ml_dtypes.bfloat16)
    return np.stack([high, low])


def angle(rows, cols):
    turns = np.outer(rows, cols) % GRID
    return turns * (2.0 * math.pi / GRID)


@functools.lru_cache
def tables():
    n = GRID
    every = np.arange(n)
    phase = angle(every, every)
    tx = np.zeros((PARTS, 8, 768))
    cosine, sine = (f(phase).reshape(PARTS, BAND, n) for f in (np.cos, np.sin))
    for at, part in ((0, cosine), (256, sine), (512, -sine)):
        tx[:, :BAND, at : at + n] = part
    tx = tx.reshape(256, 768)
    cs = np.zeros((n, 512))
    cs[:, :n] = cosine.transpose(1, 0, 2).reshape(n, n)
    cs[:, 256 : 256 + n] = sine.transpose(1, 0, 2).reshape(n, n)
    ey = np.zeros((2 * n, 256))
    eyt = np.zeros((8 * len(LIVE), 2 * n))
    for at, band in enumerate(LIVE):
        phase = angle(every, band * BAND + np.arange(BAND))
        cols = slice(8 * band, 8 * band + BAND)
        ey[:n, cols], ey[n:, cols] = np.cos(phase), np.sin(phase)
        rows = slice(8 * at, 8 * at + BAND)
        eyt[rows, :n], eyt[rows, n:] = np.cos(phase).T, np.sin(phase).T
    factor = float(n) ** -1.5
    phase = angle(np.arange(65), every)
    cosine, sine = factor * np.cos(phase), factor * np.sin(phase)
    zt = np.zeros((256, n))
    weight = np.where(np.arange(64) == 0, 1.0, 2.0)[:, None]
    zt[:64], zt[64:128] = weight * cosine[:64], -weight * sine[:64]
    for f in range(6):
        zt[128 + 16 * f : 136 + 16 * f] = 2.0 * cosine[64]
        zt[136 + 16 * f : 144 + 16 * f] = -2.0 * sine[64]
    zb = np.zeros((n, 256))
    zb[:, :64], zb[:, 64:128] = cosine[:64].T, -sine[:64].T
    for x in range(BAND):
        for a in range(3):
            zb[:, 128 + 8 * x + 2 * a] = cosine[64]
            zb[:, 128 + 8 * x + 2 * a + 1] = -sine[64]
    return tuple(halves(t) for t in (tx, cs, ey, zt, zb, eyt))


def split(value):
    high = value.astype(bf16)
    return high, (value - high.astype(f32)).astype(bf16)


def table_by_data(table, data, dims):
    high, low = split(data)
    dot = functools.partial(
        lax.dot_general, dimension_numbers=(dims, ((), ())), preferred_element_type=f32
    )
    return dot(table[0], high) + dot(table[0], low) + dot(table[1], high)


def data_by_table(data, table):
    high, low = split(data)
    dot = functools.partial(jnp.dot, preferred_element_type=f32)
    return dot(high, table[0]) + dot(low, table[0]) + dot(high, table[1])


def signed(index):
    return jnp.where(index < GRID // 2, index, index - GRID)


def pair_waves(pair, cut_ref):
    band = lax.axis_index("py") * lax.axis_size("pz") + lax.axis_index("pz")
    lane = lax.broadcasted_iota(jnp.int32, (DEPTH, 384), 1)
    upper = lane >= GRID
    kx = signed(jnp.where(upper, lane - GRID, lane))
    ky = signed(band * BAND + 2 * pair + upper.astype(jnp.int32))
    kz = lax.broadcasted_iota(jnp.int32, (DEPTH, 384), 0)
    keep = (
        (jnp.abs(kx) <= cut_ref[0]) & (jnp.abs(ky) <= cut_ref[1]) & (kz <= cut_ref[2])
    )
    waves = tuple(k.astype(f32) for k in (kx, ky, kz))
    square = waves[0] * waves[0] + waves[1] * waves[1] + waves[2] * waves[2]
    return waves, square, 1.0 / jnp.maximum(square, 1.0), keep


def project(field, waves, inverse, keep):
    normal = (waves[0] * field[0] + waves[1] * field[1] + waves[2] * field[2]) * inverse
    return [jnp.where(keep, field[a] - waves[a] * normal, 0.0) for a in range(3)]


MESH = pl.DeviceIdType.MESH
TURNS = ((1, 1), (3, 0), (2, 1), (0, 0), (1, 0), (3, 1), (2, 0), (0, 1))
OFFSETS = tuple(
    (dx, *TURNS[(k + 2 * j) % 8]) for k in range(8) for j, dx in enumerate((2, 1, 3, 0))
)


SLOTS = 31
LAST = 12
GROUPS = ((0, 13), (13, 12), (25, 6))
STRIDE = 520


def slot_of(f, x):
    return f * BAND + x + (f >= 2) * 1


def is_live(band):
    return (band < 11) | (band >= 21)


def exchange_kernel(
    cut_ref, in_hbm, tx_hbm, ey_hbm, zt_hbm, zb_hbm, eyt_hbm, out_hbm, last_hbm, stats_hbm,
    held, tx_ref, ey_ref, zt_ref, zb_ref, eyt_ref, data, data64, wide64, made, ready, arrived,
    turns, strips64, physical, back, back64, closed, closed64, top, total, stat,
    load_sems, send_sems, recv_sems, back_send, back_recv, last_send, last_recv,
    stat_send, stat_recv, own_sems,
):
    px, pz = lax.axis_index("py"), lax.axis_index("pz")
    me = px * 8 + pz
    live = is_live(me)

    def peer(offset):
        x = lax.rem(px + offset[0], 4)
        y = lax.rem(pz // 2 + offset[1], 4)
        z = lax.rem(pz % 2 + offset[2], 2)
        return x, y * 2 + z

    def flat(device):
        return device[0] * 8 + device[1]

    def place(band):
        return jnp.where(band < 11, band, band - 10)

    def remote(source, target, send, recv, device):
        return pltpu.make_async_remote_copy(
            src_ref=source,
            dst_ref=target,
            send_sem=send,
            recv_sem=recv,
            device_id={"py": device[0], "pz": device[1]},
            device_id_type=MESH,
        )

    others = [(j, offset) for j, offset in enumerate(OFFSETS) if offset != (0, 0, 0)]

    loads = [
        pltpu.make_async_copy(
            in_hbm.at[:, :, pl.ds(0, DEPTH), pl.ds(384 * p, 384)], held.at[p], load_sems.at[p]
        )
        for p in range(3)
    ]
    tabled = [
        pltpu.make_async_copy(source, target, load_sems.at[3 + k])
        for k, (source, target) in enumerate(
            ((ey_hbm, ey_ref), (zt_hbm, zt_ref), (zb_hbm, zb_ref), (eyt_hbm, eyt_ref))
        )
    ]
    quarters = [
        pltpu.make_async_copy(
            tx_hbm.at[:, :, pl.ds(low, 256)],
            tx_ref.at[:, pl.ds(256 * (k // 2), 256), pl.ds(256 * (k % 2), 256)],
            load_sems.at[7 + k],
        )
        for k, low in enumerate((0, 512, 256, 0))
    ]
    for copy in (*loads, *quarters, *tabled):
        copy.start()

    def clear(slot, carry):
        arrived[slot] = jnp.zeros((PARTS, 8, 128), f32)
        return carry

    lax.fori_loop(0, SLOTS, clear, 0)
    barrier = pltpu.get_barrier_semaphore()
    for _, offset in others:
        device = peer(offset)
        pl.semaphore_signal(
            barrier, inc=1, device_id={"py": device[0], "pz": device[1]}, device_id_type=MESH
        )

    def first_copy(group, device):
        low, count = GROUPS[group]
        return remote(
            ready.at[flat(device), pl.ds(low, count), pl.ds(0, BAND), :],
            arrived.at[pl.ds(low, count), me, pl.ds(0, BAND), :],
            send_sems.at[flat(device)],
            recv_sems.at[group, me],
            device,
        )

    lane8 = lax.broadcasted_iota(jnp.int32, (8, 128), 1)
    low6 = lax.broadcasted_iota(jnp.int32, (BAND, 128), 1) < 64

    data64[...] = jnp.zeros_like(data64)
    for pair in range(3):
        loads[pair].wait()

        @pl.when(live)
        def _():
            waves, _, inverse, keep = pair_waves(pair, cut_ref)
            parts = []
            for c in range(2):
                sol = project([held[pair, c, a] for a in range(3)], waves, inverse, keep)
                curl_y = waves[2] * sol[0] - waves[0] * sol[2]
                curl_z = waves[0] * sol[1] - waves[1] * sol[0]
                parts.append((sol, (curl_y, curl_z)))
            fields = []
            for c in range(2):
                turn = parts[1 - c][1]
                if c == 0:
                    turn = (-turn[0], -turn[1])
                sol = parts[c][0]
                fields.append((sol[1], sol[2], sol[0], turn[0], turn[1]))
            for odd in range(2):
                ky = 2 * pair + odd
                for c in range(2):
                    cols = slice(c * 256, (c + 1) * 256)
                    for f in range(5):
                        value = fields[c][f]
                        if odd:
                            value = pltpu.roll(value[:, 128:], 192, 1)
                        else:
                            value = value[:, :256]
                        low = 768 * (f // 2) + 128 * ky + 64 * (f % 2)
                        data[low : low + 64, cols] = value[:64]
                        if f == 4:
                            data[low + 64 : low + 128, cols] = value[:64]
                        data64[8 * f + ky : 8 * f + ky + 1, cols] = value[64:65]

    for copy in quarters:
        copy.wait()

    @pl.when(live)
    def _():
        high, low = split(data64[...])
        dot = functools.partial(
            lax.dot_general,
            dimension_numbers=(((1,), (1,)), ((), ())),
            preferred_element_type=f32,
        )
        wide = dot(high, tx_ref[0]) + dot(low, tx_ref[0]) + dot(high, tx_ref[1])
        for k in range(4):
            wide64[k] = wide[:, 128 * k : 128 * (k + 1)]
        for d in range(PARTS):
            tile = jnp.zeros((8, 128), f32)
            for f in range(5):
                for c in range(2):
                    spot = 16 * f + 8 * c
                    part = wide64[2 * c + d // 16, 8 * f : 8 * f + 8, :]
                    shift = (spot - 8 * (d % 16)) % 128
                    if shift:
                        part = pltpu.roll(part, shift, 1)
                    tile = jnp.where((lane8 >= spot) & (lane8 < spot + 8), part, tile)
            ready[d, LAST] = tile

    for group in range(3):

        @pl.when(live)
        def _():
            for pair in range(3):
                low = 768 * group + 256 * pair
                wide = table_by_data(tx_ref, data[low : low + 256, :], ((1,), (1,)))
                for odd in range(2):
                    at = (2 * pair + odd) * STRIDE
                    made[at : at + 512, :] = wide[:, 128 * odd : 128 * (odd + 1)]

        if group == 0:
            pl.semaphore_wait(barrier, PARTS - 1)

        @pl.when(live)
        def _():
            def fill(d, write):
                for x in range(BAND):
                    re, im = (
                        made[pl.ds(256 * c + 8 * d + x, BAND, stride=STRIDE), :] for c in range(2)
                    )
                    if group == 2:
                        write(4, x, jnp.where(low6, re, im))
                    else:
                        write(2 * group, x, jnp.where(low6, re, pltpu.roll(im, 64, 1)))
                        write(2 * group + 1, x, jnp.where(low6, pltpu.roll(re, 64, 1), im))

            for j, offset in others:
                device = peer(offset)
                d = flat(device)

                def write(f, x, value):
                    ready[d, slot_of(f, x), :BAND, :] = value

                fill(d, write)
                first_copy(group, device).start()

            def keep_own(f, x, value):
                arrived[slot_of(f, x), me, :BAND, :] = value

            fill(me, keep_own)
            if group == 0:
                arrived[LAST, me] = ready[me, LAST]

    top[...] = jnp.zeros_like(top)
    total[...] = jnp.zeros_like(total)
    for copy in tabled:
        copy.wait()

    row = lax.broadcasted_iota(jnp.int32, (256, 128), 0)
    col = lax.broadcasted_iota(jnp.int32, (256, 128), 1)
    ky = signed(row // 8 * BAND + row % 8).astype(f32)
    kz = (col % 64).astype(f32)
    sign = jnp.where(col < 64, -1.0, 1.0)
    lane = lax.broadcasted_iota(jnp.int32, (GRID, 128), 1)
    lower = lane < 64

    def await_group(group):
        low, count = GROUPS[group]
        for s in LIVE:

            @pl.when(s != me)
            def _():
                remote(
                    ready.at[0, pl.ds(low, count), pl.ds(0, BAND), :],
                    arrived.at[pl.ds(low, count), s, pl.ds(0, BAND), :],
                    send_sems.at[0],
                    recv_sems.at[group, s],
                    (px, pz),
                ).wait_recv()

    def to_grid(f, pair):
        wide = table_by_data(ey_ref, turns[...], ((1,), (0,)))
        for odd in range(2):
            x = 2 * pair + odd
            cosine = wide[:GRID, 128 * odd : 128 * (odd + 1)]
            sine = pltpu.roll(wide[GRID:, 128 * odd : 128 * (odd + 1)], 64, 1)
            near = cosine + jnp.where(lower, -sine, sine)
            mine = (lane == 16 * f + x) | (lane == 16 * f + 8 + x)
            far = jnp.where(mine, strips64[...], 0.0)
            physical[f, x] = data_by_table(jnp.concatenate([near, far], axis=1), zt_ref)

    def plain(first, last):
        def step(k, carry):
            f, pair = k // 3, k % 3
            slot = slot_of(f, 2 * pair)
            for odd in range(2):
                turns[:, 128 * odd : 128 * (odd + 1)] = arrived[slot + odd].reshape(256, 128)
            to_grid(f, pair)
            return carry

        lax.fori_loop(3 * first, 3 * last, step, 0)

    def turned(pair, carry):
        for odd in range(2):
            x = 2 * pair + odd
            d = ky * arrived[BAND + x].reshape(256, 128) - kz * arrived[x].reshape(256, 128)
            turns[:, 128 * odd : 128 * (odd + 1)] = sign * pltpu.roll(d, 64, 1)
        to_grid(5, pair)
        return carry

    await_group(0)
    tile = arrived[LAST].reshape(256, 128)
    d = ky * pltpu.roll(tile, 64, 1) - 64.0 * pltpu.roll(tile, 80, 1)
    d = jnp.where(col < 88, -pltpu.roll(d, 120, 1), pltpu.roll(d, 8, 1))
    tile = jnp.where((col >= 80) & (col < 96), d, tile)
    wide = table_by_data(ey_ref, tile, ((1,), (0,)))
    strips64[...] = wide[:GRID] + jnp.where(
        lane // 8 % 2 == 0, -pltpu.roll(wide[GRID:], 120, 1), pltpu.roll(wide[GRID:], 8, 1)
    )
    plain(0, 2)
    lax.fori_loop(0, 3, turned, 0)
    await_group(1)
    plain(2, 4)
    await_group(2)
    plain(4, 5)

    back64[...] = jnp.zeros_like(back64)

    def plane(x, carry):
        u = [physical[f, x] for f in (2, 0, 1)]
        w = [physical[f, x] for f in (5, 3, 4)]
        speed = jnp.abs(u[0]) + jnp.abs(u[1]) + jnp.abs(u[2])
        squares = u[0] * u[0] + u[1] * u[1] + u[2] * u[2]
        top[...] = jnp.maximum(top[...], jnp.max(speed.reshape(24, 8, GRID), axis=0))
        total[...] += jnp.sum(squares.reshape(24, 8, GRID), axis=0)
        q = []
        for a in range(3):
            b, c = (a + 1) % 3, (a + 2) % 3
            q.append(data_by_table(u[b] * w[c] - u[c] * w[b], zb_ref))
            near = q[a][:, :128]
            far = pltpu.roll(near, 64, 1)
            back[:GRID, 128 * a : 128 * (a + 1)] = near
            back[GRID:, 128 * a : 128 * (a + 1)] = jnp.where(lower, far, -far)
        way = lane % 8 // 2
        chosen = jnp.where(way == 0, q[0][:, 128:], jnp.where(way == 1, q[1][:, 128:], q[2][:, 128:]))
        back64[:GRID] = jnp.where(lane // 8 == x, chosen, back64[:GRID])
        wide = table_by_data(eyt_ref, back[...], ((1,), (0,)))
        for a in range(3):
            closed[a, x] = wide[:, 128 * a : 128 * (a + 1)].reshape(len(LIVE), 8, 128)
        for j, offset in others:
            device = peer(offset)

            @pl.when(is_live(flat(device)))
            def _():
                remote(
                    closed.at[:, x, place(flat(device)), pl.ds(0, BAND), :],
                    out_hbm.at[:, x, me, pl.ds(0, BAND), :],
                    back_send.at[flat(device)],
                    back_recv.at[me],
                    device,
                ).start()

        return carry

    lax.fori_loop(0, BAND, plane, 0)

    q = back64[:GRID]
    back64[GRID:] = jnp.where(lane % 2 == 0, pltpu.roll(q, 127, 1), -pltpu.roll(q, 1, 1))
    wide = table_by_data(eyt_ref, back64[...], ((1,), (0,)))
    closed64[...] = wide.reshape(len(LIVE), 8, 128)
    stat[...] = jnp.where(lane8 == 0, jnp.max(top[...]), jnp.sum(total[...]))

    def stat_copy(device):
        return remote(stat, stats_hbm.at[me], stat_send.at[flat(device)], stat_recv.at[me], device)

    for j, offset in others:
        device = peer(offset)
        stat_copy(device).start()

        @pl.when(is_live(flat(device)))
        def _():
            remote(
                closed64.at[place(flat(device))],
                last_hbm.at[me],
                last_send.at[flat(device)],
                last_recv.at[me],
                device,
            ).start()

    own = (
        pltpu.make_async_copy(
            closed.at[:, :, place(me), pl.ds(0, BAND), :],
            out_hbm.at[:, :, me, pl.ds(0, BAND), :],
            own_sems.at[0],
        ),
        pltpu.make_async_copy(closed64.at[place(me)], last_hbm.at[me], own_sems.at[1]),
    )
    stat_own = pltpu.make_async_copy(stat, stats_hbm.at[me], own_sems.at[2])
    stat_own.start()

    @pl.when(live)
    def _():
        own[0].start()
        own[1].start()
        own[0].wait()
        own[1].wait()

    stat_own.wait()

    def whole_back(source, send):
        return remote(
            closed.at[:, :, 0, pl.ds(0, BAND), :],
            out_hbm.at[:, :, source, pl.ds(0, BAND), :],
            back_send.at[send],
            back_recv.at[source],
            (px, pz),
        )

    def whole_last(source, send):
        return remote(
            closed64.at[0], last_hbm.at[source], last_send.at[send], last_recv.at[source], (px, pz)
        )

    for j, offset in others:
        device = peer(offset)
        d = flat(device)
        stat_copy(device).wait_send()

        @pl.when(live)
        def _():
            remote(
                ready.at[0, :, pl.ds(0, BAND), :],
                arrived.at[:, 0, pl.ds(0, BAND), :],
                send_sems.at[d],
                recv_sems.at[0, 0],
                (px, pz),
            ).wait_send()

        @pl.when(is_live(d))
        def _():
            whole_back(0, d).wait_send()
            whole_last(0, d).wait_send()

    for s in range(PARTS):

        @pl.when(s != me)
        def _():
            remote(stat, stats_hbm.at[s], stat_send.at[0], stat_recv.at[s], (px, pz)).wait_recv()

        @pl.when((s != me) & live)
        def _():
            whole_back(s, 0).wait_recv()
            whole_last(s, 0).wait_recv()


def close_kernel(
    cut_ref, dt_ref, power_ref, old_ref, in_ref, last_ref, stats_ref, cs_ref,
    out_ref, cfl_ref, energy_ref, terms, spectra,
):
    fastest = stats_ref[0]
    summed = stats_ref[0]
    for s in range(1, PARTS):
        fastest = jnp.maximum(fastest, stats_ref[s])
        summed = summed + stats_ref[s]
    fastest, summed = jnp.max(fastest[:, :1]), jnp.max(summed[:, 1:2])
    energy = 0.5 * summed * (1.0 / float(GRID**3))
    dt = dt_ref[0]
    cfl_ref[0] = dt * fastest * GRID * (1.0 / (2.0 * math.pi))
    energy_ref[0] = energy
    twice = jnp.maximum(jnp.full((DEPTH, 384), 2.0 * energy, f32), 0.5)
    forcing = power_ref[0] / twice
    eighth = lax.broadcasted_iota(jnp.int32, (PARTS, 128), 1) // 8

    out_ref[:, :, DEPTH:, :] = jnp.zeros((2, 3, 96 - DEPTH, 1152), f32)

    def step(pair, carry):
        window = pl.ds(pl.multiple_of(pair * 384, 128), 384)
        for odd in range(2):
            ky = 2 * pair + odd
            for a in range(3):
                terms[128 * a : 128 * (a + 1), :] = in_ref[a, pl.ds(ky, GRID, stride=8), :].T
            last = last_ref[pl.ds(ky, PARTS, stride=8), :]
            apart = jnp.concatenate(
                [jnp.where(eighth == x, last, 0.0) for x in range(BAND)], axis=0
            )
            terms[384:432, :] = apart.T[:48]
            spectra[odd] = data_by_table(terms[...], cs_ref)
        waves, square, inverse, keep = pair_waves(pair, cut_ref)

        def of_pair(a, c):
            halves = []
            for odd in range(2):
                re, im = (
                    spectra[odd, 128 * a + 64 * k : 128 * a + 64 * (k + 1), :] for k in range(2)
                )
                last = spectra[odd, 384:392, :]
                for x in range(1, BAND):
                    last = last + spectra[odd, 384 + 8 * x : 392 + 8 * x, :]
                re64, im64 = last[2 * a : 2 * a + 1], last[2 * a + 1 : 2 * a + 2]
                if c == 0:
                    value, value64 = (r[:, :256] + i[:, 256:] for r, i in ((re, im), (re64, im64)))
                else:
                    value, value64 = (i[:, :256] - r[:, 256:] for r, i in ((re, im), (re64, im64)))
                value = jnp.concatenate([value, value64, jnp.zeros((7, 256), f32)], axis=0)
                halves.append(pltpu.roll(value, 64, 1) if odd else value)
            even, odd = halves
            return jnp.concatenate([even[:, :128], even[:, 128:] + odd[:, :128], odd[:, 128:]], axis=1)

        for c in range(2):
            old = project([old_ref[c, a, :, window] for a in range(3)], waves, inverse, keep)
            forced = project([of_pair(a, c) for a in range(3)], waves, inverse, keep)
            for a in range(3):
                out_ref[c, a, :DEPTH, window] = old[a] + dt * (
                    forced[a] + forcing * old[a] - viscosity * square * old[a]
                )
        return carry

    live = is_live(lax.axis_index("py") * lax.axis_size("pz") + lax.axis_index("pz"))

    @pl.when(live)
    def _():
        lax.fori_loop(0, 3, step, 0)

    @pl.when(jnp.logical_not(live))
    def _():
        out_ref[:, :, :DEPTH, :] = jnp.zeros((2, 3, DEPTH, 1152), f32)


SM = pl.BlockSpec(memory_space=pltpu.SMEM)
ANY = pl.BlockSpec(memory_space=pl.ANY)
VMEM_BYTES = 60 * 1024 * 1024


def on_device(velocity_hat, time_step, power, cutoffs):
    tx, cs, ey, zt, zb, eyt = (jnp.asarray(t) for t in tables())
    shape = jax.ShapeDtypeStruct
    block = pl.BlockSpec((2, 3, DEPTH, 1152), lambda i: (0, 0, 0, 0))
    whole = lambda a: pl.BlockSpec(a.shape, lambda i: (0,) * a.ndim)
    dma = pltpu.SemaphoreType.DMA
    chunks, last, stats = pl.pallas_call(
        exchange_kernel,
        out_shape=(
            shape((3, BAND, PARTS, 8, 128), f32),
            shape((PARTS, 8, 128), f32),
            shape((PARTS, 8, 128), f32),
        ),
        in_specs=[SM] + [ANY] * 6,
        out_specs=(ANY, ANY, ANY),
        scratch_shapes=[
            pltpu.VMEM((3, 2, 3, DEPTH, 384), f32),
            pltpu.VMEM((2, 512, 512), bf16),
            *(pltpu.VMEM(t.shape, bf16) for t in (ey, zt, zb, eyt)),
            pltpu.VMEM((2304, 512), f32),
            pltpu.VMEM((40, 512), f32),
            pltpu.VMEM((4, 40, 128), f32),
            pltpu.VMEM((BAND * STRIDE, 128), f32),
            pltpu.VMEM((PARTS, SLOTS, 8, 128), f32),
            pltpu.VMEM((SLOTS, PARTS, 8, 128), f32),
            pltpu.VMEM((256, 256), f32),
            pltpu.VMEM((GRID, 128), f32),
            pltpu.VMEM((6, BAND, GRID, GRID), f32),
            pltpu.VMEM((2 * GRID, 384), f32),
            pltpu.VMEM((2 * GRID, 128), f32),
            pltpu.VMEM((3, BAND, len(LIVE), 8, 128), f32),
            pltpu.VMEM((len(LIVE), 8, 128), f32),
            pltpu.VMEM((8, GRID), f32),
            pltpu.VMEM((8, GRID), f32),
            pltpu.VMEM((8, 128), f32),
            dma((11,)),
            dma((PARTS,)),
            dma((3, PARTS)),
            *[dma((PARTS,))] * 6,
            dma((3,)),
        ],
        compiler_params=pltpu.CompilerParams(
            collective_id=0, has_side_effects=True, vmem_limit_bytes=VMEM_BYTES
        ),
    )(cutoffs, velocity_hat, tx, ey, zt, zb, eyt)
    chunks = chunks.reshape(3, BAND * PARTS * 8, 128)
    last = last.reshape(PARTS * 8, 128)
    return pl.pallas_call(
        close_kernel,
        grid=(1,),
        out_shape=(shape((2, 3, 96, 1152), f32), shape((1,), f32), shape((1,), f32)),
        in_specs=[SM, SM, SM, block, whole(chunks), whole(last), whole(stats), whole(cs)],
        out_specs=(pl.BlockSpec((2, 3, 96, 1152), lambda i: (0, 0, 0, 0)), SM, SM),
        scratch_shapes=[pltpu.VMEM((432, GRID), f32), pltpu.VMEM((2, 432, 512), f32)],
        compiler_params=pltpu.CompilerParams(vmem_limit_bytes=VMEM_BYTES),
    )(cutoffs, time_step, power, velocity_hat, chunks, last, stats, cs)


def solution(mesh):
    return jax.shard_map(
        on_device,
        mesh=mesh,
        in_specs=(P("member", None, None, ("py", "pz")), P("member"), P("member"), P("member")),
        out_specs=(P("member", None, None, ("py", "pz")), P("member"), P("member")),
        check_vma=False,
    )
```

time: 96.1 us -> 86.1 us (0.90)
  Pallas kernels: 93.9 us -> 83.9 us
    pallas_call x1, Pallas kernels: 85.5 us -> 75.5 us  [on_device(): pl.pallas_call(exchange_kernel, out_shape=(shape((3, BAND, PARTS, 8, 128)...]
where the time goes in v2:
time: 86.1 us; the launch traced here: 86 us
  Pallas kernels  83.9 us (97%)
  between operations  2.09 us (2%)
    pallas_call x1, Pallas kernels, on_device(): pl.pallas_call(exchange_kernel, out_shape=(shape((3, BAND, PARTS, 8, 128)...  75.5 us
    pallas_call x1, Pallas kernels, on_device(): pl.pallas_call(close_kernel, grid=(1,), out_shape=(shape((2, 3, 96, 1152)...  8.36 us

profile of v2, /device:TPU:0, one launch (start us, length us, event | category | flops | bytes accessed | tf_op | source)
XLA Modules:
  0.0 86.0 jit_solution(15036374604911849645)
XLA Ops:
  1.9 75.5 %shard_map.121 = (f32[3,6,32,8,128]{4,3,2,1,0:T(8,128)}, f32[32,8,128]{2,1,0:T(8,128)}, f32[32,8,128]{2,1,0:T(8,128)}) custom-call(s32[3]{0:T(128)} %cut_ref.3, f32[2,3,96,1152]{3,2,1,0:T(8,128)} %old_ref.1, bf16[2,256,768]{2,1,0:T(8,128)(2,1)} %constant.12.clone.tx_hbm, bf16[2,384,256]{2,1,0:T(8,128)(2,1)} %constant.14.clone.ey_hbm, ...), custom_call_target="tpu_custom_call" | custom-call | tf_op jit(solution)/shard_map/pallas_call | solution.py:612
  77.4 8.4 %shard_map.122 = (f32[2,3,96,1152]{3,2,1,0:T(8,128)}, f32[1]{0:T(128)}, f32[1]{0:T(128)}) custom-call(s32[3]{0:T(128)} %cut_ref.3, f32[1]{0:T(128)S(6)} %copy.13.dt_ref, f32[1]{0:T(128)S(6)} %copy.14.power_ref, f32[2,3,96,1152]{3,2,1,0:T(8,128)} %old_ref.1, f32[3,1536,128]{2,1,0:T(8,128)} %bitcast.2, f32[256,128]{1,0:T(8,128)} %bitcast.3, ...), custom_call_target="tpu_custom_call" | custom-call | tf_op jit(solution)/shard_map/pallas_call | solution.py:653

commit v3 on v2

--- a/solution.py
+++ b/solution.py
@@ -121,13 +121,11 @@
 
 
 SLOTS = 31
-LAST = 12
-GROUPS = ((0, 13), (13, 12), (25, 6))
 STRIDE = 520
 
 
 def slot_of(f, x):
-    return f * BAND + x + (f >= 2) * 1
+    return 1 + 5 * x + f
 
 
 def is_live(band):
@@ -138,7 +136,7 @@
     cut_ref, in_hbm, tx_hbm, ey_hbm, zt_hbm, zb_hbm, eyt_hbm, out_hbm, last_hbm, stats_hbm,
     held, tx_ref, ey_ref, zt_ref, zb_ref, eyt_ref, data, data64, wide64, made, ready, arrived,
     turns, strips64, physical, back, back64, closed, closed64, top, total, stat,
-    load_sems, send_sems, recv_sems, back_send, back_recv, last_send, last_recv,
+    load_sems, send_sems, recv_sems, send64, recv64, back_send, back_recv, last_send, last_recv,
     stat_send, stat_recv, own_sems,
 ):
     px, pz = lax.axis_index("py"), lax.axis_index("pz")
@@ -204,13 +202,13 @@
             barrier, inc=1, device_id={"py": device[0], "pz": device[1]}, device_id_type=MESH
         )
 
-    def first_copy(group, device):
-        low, count = GROUPS[group]
+    def first_copy(x, device):
+        slots = pl.ds(1 + 5 * x, 5)
         return remote(
-            ready.at[flat(device), pl.ds(low, count), pl.ds(0, BAND), :],
-            arrived.at[pl.ds(low, count), me, pl.ds(0, BAND), :],
+            ready.at[flat(device), slots, pl.ds(0, BAND), :],
+            arrived.at[slots, me, pl.ds(0, BAND), :],
             send_sems.at[flat(device)],
-            recv_sems.at[group, me],
+            recv_sems.at[x, me],
             device,
         )
 
@@ -277,51 +275,61 @@
                     if shift:
                         part = pltpu.roll(part, shift, 1)
                     tile = jnp.where((lane8 >= spot) & (lane8 < spot + 8), part, tile)
-            ready[d, LAST] = tile
-
-    for group in range(3):
-
-        @pl.when(live)
-        def _():
+            ready[d, 0] = tile
+
+        for group in range(3):
             for pair in range(3):
                 low = 768 * group + 256 * pair
                 wide = table_by_data(tx_ref, data[low : low + 256, :], ((1,), (1,)))
                 for odd in range(2):
                     at = (2 * pair + odd) * STRIDE
-                    made[at : at + 512, :] = wide[:, 128 * odd : 128 * (odd + 1)]
-
-        if group == 0:
-            pl.semaphore_wait(barrier, PARTS - 1)
-
-        @pl.when(live)
-        def _():
+                    made[group, at : at + 512, :] = wide[:, 128 * odd : 128 * (odd + 1)]
+
+    pl.semaphore_wait(barrier, PARTS - 1)
+
+    @pl.when(live)
+    def _():
+        for j, offset in others:
+            device = peer(offset)
+            remote(
+                ready.at[flat(device), 0],
+                arrived.at[0, me],
+                send64.at[flat(device)],
+                recv64.at[me],
+                device,
+            ).start()
+        arrived[0, me] = ready[me, 0]
+
+        def spread(x, carry):
             def fill(d, write):
-                for x in range(BAND):
+                for group in range(3):
                     re, im = (
-                        made[pl.ds(256 * c + 8 * d + x, BAND, stride=STRIDE), :] for c in range(2)
+                        made[group, pl.ds(256 * c + 8 * d + x, BAND, stride=STRIDE), :]
+                        for c in range(2)
                     )
                     if group == 2:
-                        write(4, x, jnp.where(low6, re, im))
+                        write(4, jnp.where(low6, re, im))
                     else:
-                        write(2 * group, x, jnp.where(low6, re, pltpu.roll(im, 64, 1)))
-                        write(2 * group + 1, x, jnp.where(low6, pltpu.roll(re, 64, 1), im))
+                        write(2 * group, jnp.where(low6, re, pltpu.roll(im, 64, 1)))
+                        write(2 * group + 1, jnp.where(low6, pltpu.roll(re, 64, 1), im))
 
             for j, offset in others:
                 device = peer(offset)
                 d = flat(device)
 
-                def write(f, x, value):
+                def write(f, value):
                     ready[d, slot_of(f, x), :BAND, :] = value
 
                 fill(d, write)
-                first_copy(group, device).start()
-
-            def keep_own(f, x, value):
+                first_copy(x, device).start()
+
+            def keep_own(f, value):
                 arrived[slot_of(f, x), me, :BAND, :] = value
 
             fill(me, keep_own)
-            if group == 0:
-                arrived[LAST, me] = ready[me, LAST]
+            return carry
+
+        lax.fori_loop(0, BAND, spread, 0)
 
     top[...] = jnp.zeros_like(top)
     total[...] = jnp.zeros_like(total)
@@ -336,52 +344,28 @@
     lane = lax.broadcasted_iota(jnp.int32, (GRID, 128), 1)
     lower = lane < 64
 
-    def await_group(group):
-        low, count = GROUPS[group]
-        for s in LIVE:
-
-            @pl.when(s != me)
-            def _():
-                remote(
-                    ready.at[0, pl.ds(low, count), pl.ds(0, BAND), :],
-                    arrived.at[pl.ds(low, count), s, pl.ds(0, BAND), :],
-                    send_sems.at[0],
-                    recv_sems.at[group, s],
-                    (px, pz),
-                ).wait_recv()
-
-    def to_grid(f, pair):
+    def to_grid(x, pair, tiles):
+        for odd in range(2):
+            turns[:, 128 * odd : 128 * (odd + 1)] = tiles[odd]
         wide = table_by_data(ey_ref, turns[...], ((1,), (0,)))
         for odd in range(2):
-            x = 2 * pair + odd
+            f = 2 * pair + odd
             cosine = wide[:GRID, 128 * odd : 128 * (odd + 1)]
             sine = pltpu.roll(wide[GRID:, 128 * odd : 128 * (odd + 1)], 64, 1)
             near = cosine + jnp.where(lower, -sine, sine)
             mine = (lane == 16 * f + x) | (lane == 16 * f + 8 + x)
             far = jnp.where(mine, strips64[...], 0.0)
-            physical[f, x] = data_by_table(jnp.concatenate([near, far], axis=1), zt_ref)
-
-    def plain(first, last):
-        def step(k, carry):
-            f, pair = k // 3, k % 3
-            slot = slot_of(f, 2 * pair)
-            for odd in range(2):
-                turns[:, 128 * odd : 128 * (odd + 1)] = arrived[slot + odd].reshape(256, 128)
-            to_grid(f, pair)
-            return carry
-
-        lax.fori_loop(3 * first, 3 * last, step, 0)
-
-    def turned(pair, carry):
-        for odd in range(2):
-            x = 2 * pair + odd
-            d = ky * arrived[BAND + x].reshape(256, 128) - kz * arrived[x].reshape(256, 128)
-            turns[:, 128 * odd : 128 * (odd + 1)] = sign * pltpu.roll(d, 64, 1)
-        to_grid(5, pair)
-        return carry
-
-    await_group(0)
-    tile = arrived[LAST].reshape(256, 128)
+            physical[f] = data_by_table(jnp.concatenate([near, far], axis=1), zt_ref)
+
+    for s in LIVE:
+
+        @pl.when(s != me)
+        def _():
+            remote(
+                ready.at[0, 0], arrived.at[0, s], send64.at[0], recv64.at[s], (px, pz)
+            ).wait_recv()
+
+    tile = arrived[0].reshape(256, 128)
     d = ky * pltpu.roll(tile, 64, 1) - 64.0 * pltpu.roll(tile, 80, 1)
     d = jnp.where(col < 88, -pltpu.roll(d, 120, 1), pltpu.roll(d, 8, 1))
     tile = jnp.where((col >= 80) & (col < 96), d, tile)
@@ -389,18 +373,29 @@
     strips64[...] = wide[:GRID] + jnp.where(
         lane // 8 % 2 == 0, -pltpu.roll(wide[GRID:], 120, 1), pltpu.roll(wide[GRID:], 8, 1)
     )
-    plain(0, 2)
-    lax.fori_loop(0, 3, turned, 0)
-    await_group(1)
-    plain(2, 4)
-    await_group(2)
-    plain(4, 5)
-
     back64[...] = jnp.zeros_like(back64)
 
     def plane(x, carry):
-        u = [physical[f, x] for f in (2, 0, 1)]
-        w = [physical[f, x] for f in (5, 3, 4)]
+        for s in LIVE:
+
+            @pl.when(s != me)
+            def _():
+                slots = pl.ds(1 + 5 * x, 5)
+                remote(
+                    ready.at[0, slots, pl.ds(0, BAND), :],
+                    arrived.at[slots, s, pl.ds(0, BAND), :],
+                    send_sems.at[0],
+                    recv_sems.at[x, s],
+                    (px, pz),
+                ).wait_recv()
+
+        tiles = [arrived[slot_of(f, x)].reshape(256, 128) for f in range(2)]
+        to_grid(x, 0, tiles)
+        turned = sign * pltpu.roll(ky * tiles[1] - kz * tiles[0], 64, 1)
+        to_grid(x, 1, [arrived[slot_of(f, x)].reshape(256, 128) for f in (2, 3)])
+        to_grid(x, 2, [arrived[slot_of(4, x)].reshape(256, 128), turned])
+        u = [physical[f] for f in (2, 0, 1)]
+        w = [physical[f] for f in (5, 3, 4)]
         speed = jnp.abs(u[0]) + jnp.abs(u[1]) + jnp.abs(u[2])
         squares = u[0] * u[0] + u[1] * u[1] + u[2] * u[2]
         top[...] = jnp.maximum(top[...], jnp.max(speed.reshape(24, 8, GRID), axis=0))
@@ -501,11 +496,14 @@
         @pl.when(live)
         def _():
             remote(
-                ready.at[0, :, pl.ds(0, BAND), :],
-                arrived.at[:, 0, pl.ds(0, BAND), :],
+                ready.at[0, pl.ds(1, SLOTS - 1), pl.ds(0, BAND), :],
+                arrived.at[pl.ds(1, SLOTS - 1), 0, pl.ds(0, BAND), :],
                 send_sems.at[d],
                 recv_sems.at[0, 0],
                 (px, pz),
+            ).wait_send()
+            remote(
+                ready.at[0, 0], arrived.at[0, 0], send64.at[d], recv64.at[0], (px, pz)
             ).wait_send()
 
         @pl.when(is_live(d))
@@ -543,10 +541,13 @@
     forcing = power_ref[0] / twice
     eighth = lax.broadcasted_iota(jnp.int32, (PARTS, 128), 1) // 8
 
-    out_ref[:, :, DEPTH:, :] = jnp.zeros((2, 3, 96 - DEPTH, 1152), f32)
-
-    def step(pair, carry):
-        window = pl.ds(pl.multiple_of(pair * 384, 128), 384)
+    out_ref[:, :, DEPTH:, :] = jnp.zeros((2, 3, 96 - DEPTH, 384), f32)
+
+    pair = pl.program_id(0)
+    live = is_live(lax.axis_index("py") * lax.axis_size("pz") + lax.axis_index("pz"))
+
+    @pl.when(live)
+    def _():
         for odd in range(2):
             ky = 2 * pair + odd
             for a in range(3):
@@ -579,23 +580,16 @@
             return jnp.concatenate([even[:, :128], even[:, 128:] + odd[:, :128], odd[:, 128:]], axis=1)
 
         for c in range(2):
-            old = project([old_ref[c, a, :, window] for a in range(3)], waves, inverse, keep)
+            old = project([old_ref[c, a, :, :] for a in range(3)], waves, inverse, keep)
             forced = project([of_pair(a, c) for a in range(3)], waves, inverse, keep)
             for a in range(3):
-                out_ref[c, a, :DEPTH, window] = old[a] + dt * (
+                out_ref[c, a, :DEPTH, :] = old[a] + dt * (
                     forced[a] + forcing * old[a] - viscosity * square * old[a]
                 )
-        return carry
-
-    live = is_live(lax.axis_index("py") * lax.axis_size("pz") + lax.axis_index("pz"))
-
-    @pl.when(live)
-    def _():
-        lax.fori_loop(0, 3, step, 0)
 
     @pl.when(jnp.logical_not(live))
     def _():
-        out_ref[:, :, :DEPTH, :] = jnp.zeros((2, 3, DEPTH, 1152), f32)
+        out_ref[:, :, :DEPTH, :] = jnp.zeros((2, 3, DEPTH, 384), f32)
 
 
 SM = pl.BlockSpec(memory_space=pltpu.SMEM)
@@ -606,7 +600,7 @@
 def on_device(velocity_hat, time_step, power, cutoffs):
     tx, cs, ey, zt, zb, eyt = (jnp.asarray(t) for t in tables())
     shape = jax.ShapeDtypeStruct
-    block = pl.BlockSpec((2, 3, DEPTH, 1152), lambda i: (0, 0, 0, 0))
+    block = pl.BlockSpec((2, 3, DEPTH, 384), lambda i: (0, 0, 0, i))
     whole = lambda a: pl.BlockSpec(a.shape, lambda i: (0,) * a.ndim)
     dma = pltpu.SemaphoreType.DMA
     chunks, last, stats = pl.pallas_call(
@@ -625,12 +619,12 @@
             pltpu.VMEM((2304, 512), f32),
             pltpu.VMEM((40, 512), f32),
             pltpu.VMEM((4, 40, 128), f32),
-            pltpu.VMEM((BAND * STRIDE, 128), f32),
+            pltpu.VMEM((3, BAND * STRIDE, 128), f32),
             pltpu.VMEM((PARTS, SLOTS, 8, 128), f32),
             pltpu.VMEM((SLOTS, PARTS, 8, 128), f32),
             pltpu.VMEM((256, 256), f32),
             pltpu.VMEM((GRID, 128), f32),
-            pltpu.VMEM((6, BAND, GRID, GRID), f32),
+            pltpu.VMEM((6, GRID, GRID), f32),
             pltpu.VMEM((2 * GRID, 384), f32),
             pltpu.VMEM((2 * GRID, 128), f32),
             pltpu.VMEM((3, BAND, len(LIVE), 8, 128), f32),
@@ -640,8 +634,8 @@
             pltpu.VMEM((8, 128), f32),
             dma((11,)),
             dma((PARTS,)),
-            dma((3, PARTS)),
-            *[dma((PARTS,))] * 6,
+            dma((BAND, PARTS)),
+            *[dma((PARTS,))] * 8,
             dma((3,)),
         ],
         compiler_params=pltpu.CompilerParams(
@@ -652,10 +646,10 @@
     last = last.reshape(PARTS * 8, 128)
     return pl.pallas_call(
         close_kernel,
-        grid=(1,),
+        grid=(3,),
         out_shape=(shape((2, 3, 96, 1152), f32), shape((1,), f32), shape((1,), f32)),
         in_specs=[SM, SM, SM, block, whole(chunks), whole(last), whole(stats), whole(cs)],
-        out_specs=(pl.BlockSpec((2, 3, 96, 1152), lambda i: (0, 0, 0, 0)), SM, SM),
+        out_specs=(pl.BlockSpec((2, 3, 96, 384), lambda i: (0, 0, 0, i)), SM, SM),
         scratch_shapes=[pltpu.VMEM((432, GRID), f32), pltpu.VMEM((2, 432, 512), f32)],
         compiler_params=pltpu.CompilerParams(vmem_limit_bytes=VMEM_BYTES),
     )(cutoffs, time_step, power, velocity_hat, chunks, last, stats, cs)

time: 86.1 us -> 83.5 us (0.970)
  Pallas kernels: 83.9 us -> 81.4 us
    pallas_call x1, Pallas kernels: 75.5 us -> 73.5 us  [on_device(): pl.pallas_call(exchange_kernel, out_shape=(shape((3, BAND, PARTS, 8, 128)...]
where the time goes in v3:
time: 83.5 us; the launch traced here: 83.3 us
  Pallas kernels  81.4 us (97%)
  between operations  1.93 us (2%)
    pallas_call x1, Pallas kernels, on_device(): pl.pallas_call(exchange_kernel, out_shape=(shape((3, BAND, PARTS, 8, 128)...  73.5 us
    pallas_call x1, Pallas kernels, on_device(): pl.pallas_call(close_kernel, grid=(3,), out_shape=(shape((2, 3, 96, 1152)...  7.83 us

profile of v3, /device:TPU:0, one launch (start us, length us, event | category | flops | bytes accessed | tf_op | source)
XLA Modules:
  0.0 83.3 jit_solution(9671097820275799930)
XLA Ops:
  1.9 73.5 %shard_map.121 = (f32[3,6,32,8,128]{4,3,2,1,0:T(8,128)}, f32[32,8,128]{2,1,0:T(8,128)}, f32[32,8,128]{2,1,0:T(8,128)}) custom-call(s32[3]{0:T(128)} %cut_ref.3, f32[2,3,96,1152]{3,2,1,0:T(8,128)} %old_ref.1, bf16[2,256,768]{2,1,0:T(8,128)(2,1)} %constant.12.clone.tx_hbm, bf16[2,384,256]{2,1,0:T(8,128)(2,1)} %constant.14.clone.ey_hbm, ...), custom_call_target="tpu_custom_call" | custom-call | tf_op jit(solution)/shard_map/pallas_call | solution.py:606
  75.5 7.8 %shard_map.122 = (f32[2,3,96,1152]{3,2,1,0:T(8,128)}, f32[1]{0:T(128)}, f32[1]{0:T(128)}) custom-call(s32[3]{0:T(128)} %cut_ref.3, f32[1]{0:T(128)S(6)} %copy.13.dt_ref, f32[1]{0:T(128)S(6)} %copy.14.power_ref, f32[2,3,96,1152]{3,2,1,0:T(8,128)} %old_ref.1, f32[3,1536,128]{2,1,0:T(8,128)} %bitcast.2, f32[256,128]{1,0:T(8,128)} %bitcast.3, ...), custom_call_target="tpu_custom_call" | custom-call | tf_op jit(solution)/shard_map/pallas_call | solution.py:647

commit v4 on v3

--- a/solution.py
+++ b/solution.py
@@ -136,8 +136,7 @@
     cut_ref, in_hbm, tx_hbm, ey_hbm, zt_hbm, zb_hbm, eyt_hbm, out_hbm, last_hbm, stats_hbm,
     held, tx_ref, ey_ref, zt_ref, zb_ref, eyt_ref, data, data64, wide64, made, ready, arrived,
     turns, strips64, physical, back, back64, closed, closed64, top, total, stat,
-    load_sems, send_sems, recv_sems, send64, recv64, back_send, back_recv, last_send, last_recv,
-    stat_send, stat_recv, own_sems,
+    load_sems, send_sems, recv_sems, back_sems, own_sems,
 ):
     px, pz = lax.axis_index("py"), lax.axis_index("pz")
     me = px * 8 + pz
@@ -207,8 +206,8 @@
         return remote(
             ready.at[flat(device), slots, pl.ds(0, BAND), :],
             arrived.at[slots, me, pl.ds(0, BAND), :],
-            send_sems.at[flat(device)],
-            recv_sems.at[x, me],
+            send_sems.at[0],
+            recv_sems.at[x],
             device,
         )
 
@@ -294,8 +293,8 @@
             remote(
                 ready.at[flat(device), 0],
                 arrived.at[0, me],
-                send64.at[flat(device)],
-                recv64.at[me],
+                send_sems.at[1],
+                recv_sems.at[BAND],
                 device,
             ).start()
         arrived[0, me] = ready[me, 0]
@@ -357,14 +356,15 @@
             far = jnp.where(mine, strips64[...], 0.0)
             physical[f] = data_by_table(jnp.concatenate([near, far], axis=1), zt_ref)
 
-    for s in LIVE:
-
-        @pl.when(s != me)
-        def _():
-            remote(
-                ready.at[0, 0], arrived.at[0, s], send64.at[0], recv64.at[s], (px, pz)
-            ).wait_recv()
-
+    def from_live(await_count):
+        pl.when(live)(lambda: await_count(len(LIVE) - 1))
+        pl.when(jnp.logical_not(live))(lambda: await_count(len(LIVE)))
+
+    def await_last(count):
+        part = arrived.at[0, pl.ds(0, count)]
+        remote(part, part, send_sems.at[1], recv_sems.at[BAND], (px, pz)).wait_recv()
+
+    from_live(await_last)
     tile = arrived[0].reshape(256, 128)
     d = ky * pltpu.roll(tile, 64, 1) - 64.0 * pltpu.roll(tile, 80, 1)
     d = jnp.where(col < 88, -pltpu.roll(d, 120, 1), pltpu.roll(d, 8, 1))
@@ -376,19 +376,11 @@
     back64[...] = jnp.zeros_like(back64)
 
     def plane(x, carry):
-        for s in LIVE:
-
-            @pl.when(s != me)
-            def _():
-                slots = pl.ds(1 + 5 * x, 5)
-                remote(
-                    ready.at[0, slots, pl.ds(0, BAND), :],
-                    arrived.at[slots, s, pl.ds(0, BAND), :],
-                    send_sems.at[0],
-                    recv_sems.at[x, s],
-                    (px, pz),
-                ).wait_recv()
-
+        def await_plane(count):
+            part = arrived.at[pl.ds(1 + 5 * x, 5), pl.ds(0, count), pl.ds(0, BAND), :]
+            remote(part, part, send_sems.at[0], recv_sems.at[x], (px, pz)).wait_recv()
+
+        from_live(await_plane)
         tiles = [arrived[slot_of(f, x)].reshape(256, 128) for f in range(2)]
         to_grid(x, 0, tiles)
         turned = sign * pltpu.roll(ky * tiles[1] - kz * tiles[0], 64, 1)
@@ -422,8 +414,8 @@
                 remote(
                     closed.at[:, x, place(flat(device)), pl.ds(0, BAND), :],
                     out_hbm.at[:, x, me, pl.ds(0, BAND), :],
-                    back_send.at[flat(device)],
-                    back_recv.at[me],
+                    back_sems.at[0],
+                    back_sems.at[1],
                     device,
                 ).start()
 
@@ -438,7 +430,7 @@
     stat[...] = jnp.where(lane8 == 0, jnp.max(top[...]), jnp.sum(total[...]))
 
     def stat_copy(device):
-        return remote(stat, stats_hbm.at[me], stat_send.at[flat(device)], stat_recv.at[me], device)
+        return remote(stat, stats_hbm.at[me], back_sems.at[2], back_sems.at[3], device)
 
     for j, offset in others:
         device = peer(offset)
@@ -449,8 +441,8 @@
             remote(
                 closed64.at[place(flat(device))],
                 last_hbm.at[me],
-                last_send.at[flat(device)],
-                last_recv.at[me],
+                back_sems.at[4],
+                back_sems.at[5],
                 device,
             ).start()
 
@@ -474,53 +466,28 @@
 
     stat_own.wait()
 
-    def whole_back(source, send):
-        return remote(
-            closed.at[:, :, 0, pl.ds(0, BAND), :],
-            out_hbm.at[:, :, source, pl.ds(0, BAND), :],
-            back_send.at[send],
-            back_recv.at[source],
-            (px, pz),
-        )
-
-    def whole_last(source, send):
-        return remote(
-            closed64.at[0], last_hbm.at[source], last_send.at[send], last_recv.at[source], (px, pz)
-        )
-
-    for j, offset in others:
-        device = peer(offset)
-        d = flat(device)
-        stat_copy(device).wait_send()
-
-        @pl.when(live)
-        def _():
-            remote(
-                ready.at[0, pl.ds(1, SLOTS - 1), pl.ds(0, BAND), :],
-                arrived.at[pl.ds(1, SLOTS - 1), 0, pl.ds(0, BAND), :],
-                send_sems.at[d],
-                recv_sems.at[0, 0],
-                (px, pz),
-            ).wait_send()
-            remote(
-                ready.at[0, 0], arrived.at[0, 0], send64.at[d], recv64.at[0], (px, pz)
-            ).wait_send()
-
-        @pl.when(is_live(d))
-        def _():
-            whole_back(0, d).wait_send()
-            whole_last(0, d).wait_send()
-
-    for s in range(PARTS):
-
-        @pl.when(s != me)
-        def _():
-            remote(stat, stats_hbm.at[s], stat_send.at[0], stat_recv.at[s], (px, pz)).wait_recv()
-
-        @pl.when((s != me) & live)
-        def _():
-            whole_back(s, 0).wait_recv()
-            whole_last(s, 0).wait_recv()
+    def sent(part, sem):
+        remote(part, part, sem, recv_sems.at[0], (px, pz)).wait_send()
+
+    def came(part, sem):
+        remote(part, part, send_sems.at[0], sem, (px, pz)).wait_recv()
+
+    rest = pl.ds(0, PARTS - 1)
+
+    def await_sent(count):
+        sent(closed.at[:, :, pl.ds(0, count), pl.ds(0, BAND), :], back_sems.at[0])
+        sent(closed64.at[pl.ds(0, count)], back_sems.at[4])
+
+    from_live(await_sent)
+    sent(arrived.at[0, rest], back_sems.at[2])
+    came(stats_hbm.at[rest], back_sems.at[3])
+
+    @pl.when(live)
+    def _():
+        sent(ready.at[rest, pl.ds(1, SLOTS - 1), pl.ds(0, BAND), :], send_sems.at[0])
+        sent(ready.at[rest, 0], send_sems.at[1])
+        came(out_hbm.at[:, :, rest, pl.ds(0, BAND), :], back_sems.at[1])
+        came(last_hbm.at[rest], back_sems.at[5])
 
 
 def close_kernel(
@@ -633,9 +600,9 @@
             pltpu.VMEM((8, GRID), f32),
             pltpu.VMEM((8, 128), f32),
             dma((11,)),
-            dma((PARTS,)),
-            dma((BAND, PARTS)),
-            *[dma((PARTS,))] * 8,
+            dma((2,)),
+            dma((BAND + 1,)),
+            dma((6,)),
             dma((3,)),
         ],
         compiler_params=pltpu.CompilerParams(

time: 83.5 us -> 79.3 us (0.950)
  Pallas kernels: 81.4 us -> 77.2 us
    pallas_call x1, Pallas kernels: 73.5 us -> 69.4 us  [on_device(): pl.pallas_call(exchange_kernel, out_shape=(shape((3, BAND, PARTS, 8, 128)...]
where the time goes in v4:
time: 79.3 us; the launch traced here: 79.1 us
  Pallas kernels  77.2 us (97%)
  between operations  1.93 us (2%)
    pallas_call x1, Pallas kernels, on_device(): pl.pallas_call(exchange_kernel, out_shape=(shape((3, BAND, PARTS, 8, 128)...  69.4 us
    pallas_call x1, Pallas kernels, on_device(): pl.pallas_call(close_kernel, grid=(3,), out_shape=(shape((2, 3, 96, 1152)...  7.83 us

profile of v4, /device:TPU:0, one launch (start us, length us, event | category | flops | bytes accessed | tf_op | source)
XLA Modules:
  0.0 79.1 jit_solution(8573879928361337666)
XLA Ops:
  1.9 69.4 %shard_map.121 = (f32[3,6,32,8,128]{4,3,2,1,0:T(8,128)}, f32[32,8,128]{2,1,0:T(8,128)}, f32[32,8,128]{2,1,0:T(8,128)}) custom-call(s32[3]{0:T(128)} %cut_ref.3, f32[2,3,96,1152]{3,2,1,0:T(8,128)} %old_ref.1, bf16[2,256,768]{2,1,0:T(8,128)(2,1)} %constant.12.clone.tx_hbm, bf16[2,384,256]{2,1,0:T(8,128)(2,1)} %constant.14.clone.ey_hbm, ...), custom_call_target="tpu_custom_call" | custom-call | tf_op jit(solution)/shard_map/pallas_call | solution.py:573
  71.3 7.8 %shard_map.122 = (f32[2,3,96,1152]{3,2,1,0:T(8,128)}, f32[1]{0:T(128)}, f32[1]{0:T(128)}) custom-call(s32[3]{0:T(128)} %cut_ref.3, f32[1]{0:T(128)S(6)} %copy.13.dt_ref, f32[1]{0:T(128)S(6)} %copy.14.power_ref, f32[2,3,96,1152]{3,2,1,0:T(8,128)} %old_ref.1, f32[3,1536,128]{2,1,0:T(8,128)} %bitcast.2, f32[256,128]{1,0:T(8,128)} %bitcast.3, ...), custom_call_target="tpu_custom_call" | custom-call | tf_op jit(solution)/shard_map/pallas_call | solution.py:614

commit v5 on v4

--- a/solution.py
+++ b/solution.py
@@ -36,14 +36,16 @@
     n = GRID
     every = np.arange(n)
     phase = angle(every, every)
-    tx = np.zeros((PARTS, 8, 768))
-    cosine, sine = (f(phase).reshape(PARTS, BAND, n) for f in (np.cos, np.sin))
-    for at, part in ((0, cosine), (256, sine), (512, -sine)):
-        tx[:, :BAND, at : at + n] = part
-    tx = tx.reshape(256, 768)
-    cs = np.zeros((n, 512))
-    cs[:, :n] = cosine.transpose(1, 0, 2).reshape(n, n)
-    cs[:, 256 : 256 + n] = sine.transpose(1, 0, 2).reshape(n, n)
+    near = np.where(np.arange(128) <= 64, np.arange(128), np.arange(128) + 64)
+    phase = angle(every, near)
+    tx = np.zeros((PARTS, 8, 384))
+    cosine, sine = (f(phase).reshape(PARTS, BAND, 128) for f in (np.cos, np.sin))
+    for at, part in ((0, cosine), (128, sine), (256, -sine)):
+        tx[:, :BAND, at : at + 128] = part
+    tx = tx.reshape(256, 384)
+    cs = np.zeros((n, 256))
+    cs[:, :128] = cosine.transpose(1, 0, 2).reshape(n, 128)
+    cs[:, 128:] = sine.transpose(1, 0, 2).reshape(n, 128)
     ey = np.zeros((2 * n, 256))
     eyt = np.zeros((8 * len(LIVE), 2 * n))
     for at, band in enumerate(LIVE):
@@ -180,11 +182,11 @@
     ]
     quarters = [
         pltpu.make_async_copy(
-            tx_hbm.at[:, :, pl.ds(low, 256)],
-            tx_ref.at[:, pl.ds(256 * (k // 2), 256), pl.ds(256 * (k % 2), 256)],
+            tx_hbm.at[:, :, pl.ds(low, 128)],
+            tx_ref.at[:, pl.ds(256 * (k // 2), 256), pl.ds(128 * (k % 2), 128)],
             load_sems.at[7 + k],
         )
-        for k, low in enumerate((0, 512, 256, 0))
+        for k, low in enumerate((0, 256, 128, 0))
     ]
     for copy in (*loads, *quarters, *tabled):
         copy.start()
@@ -234,36 +236,49 @@
                     turn = (-turn[0], -turn[1])
                 sol = parts[c][0]
                 fields.append((sol[1], sol[2], sol[0], turn[0], turn[1]))
+            spot = lax.broadcasted_iota(jnp.int32, (DEPTH, 128), 1)
             for odd in range(2):
                 ky = 2 * pair + odd
                 for c in range(2):
-                    cols = slice(c * 256, (c + 1) * 256)
                     for f in range(5):
                         value = fields[c][f]
                         if odd:
-                            value = pltpu.roll(value[:, 128:], 192, 1)
+                            first = pltpu.roll(value[:, 128:256], 64, 1)
+                            last = value[:, 256:]
+                            edge = pltpu.roll(last, 64, 1)
                         else:
-                            value = value[:, :256]
+                            first = edge = value[:, :128]
+                            last = pltpu.roll(value[:, 128:256], 64, 1)
+                        base = jnp.where(spot < 64, first, last)
+                        both = (
+                            jnp.where(spot == 64, edge + last, base),
+                            jnp.where(spot == 64, edge - last, base),
+                        )
                         low = 768 * (f // 2) + 128 * ky + 64 * (f % 2)
-                        data[low : low + 64, cols] = value[:64]
-                        if f == 4:
-                            data[low + 64 : low + 128, cols] = value[:64]
-                        data64[8 * f + ky : 8 * f + ky + 1, cols] = value[64:65]
+                        cols = slice(128 * c, 128 * (c + 1))
+                        for k in range(2):
+                            part = both[(k + c) % 2]
+                            data[k, low : low + 64, cols] = part[:64]
+                            if f == 4:
+                                data[k, low + 64 : low + 128, cols] = part[:64]
+                            data64[k, 8 * f + ky : 8 * f + ky + 1, cols] = part[64:65]
 
     for copy in quarters:
         copy.wait()
 
     @pl.when(live)
     def _():
-        high, low = split(data64[...])
         dot = functools.partial(
             lax.dot_general,
             dimension_numbers=(((1,), (1,)), ((), ())),
             preferred_element_type=f32,
         )
-        wide = dot(high, tx_ref[0]) + dot(low, tx_ref[0]) + dot(high, tx_ref[1])
-        for k in range(4):
-            wide64[k] = wide[:, 128 * k : 128 * (k + 1)]
+        for c in range(2):
+            high, low = split(data64[c])
+            fine, rest = (tx_ref[k, 256 * c : 256 * (c + 1), :] for k in range(2))
+            wide = dot(high, fine) + dot(low, fine) + dot(high, rest)
+            for k in range(2):
+                wide64[2 * c + k] = wide[:, 128 * k : 128 * (k + 1)]
         for d in range(PARTS):
             tile = jnp.zeros((8, 128), f32)
             for f in range(5):
@@ -279,10 +294,15 @@
         for group in range(3):
             for pair in range(3):
                 low = 768 * group + 256 * pair
-                wide = table_by_data(tx_ref, data[low : low + 256, :], ((1,), (1,)))
-                for odd in range(2):
-                    at = (2 * pair + odd) * STRIDE
-                    made[group, at : at + 512, :] = wide[:, 128 * odd : 128 * (odd + 1)]
+                for c in range(2):
+                    wide = table_by_data(
+                        tx_ref[:, 256 * c : 256 * (c + 1), :],
+                        data[c, low : low + 256, :],
+                        ((1,), (1,)),
+                    )
+                    for odd in range(2):
+                        at = (2 * pair + odd) * STRIDE + 256 * c
+                        made[group, at : at + 256, :] = wide[:, 128 * odd : 128 * (odd + 1)]
 
     pl.semaphore_wait(barrier, PARTS - 1)
 
@@ -527,8 +547,10 @@
             spectra[odd] = data_by_table(terms[...], cs_ref)
         waves, square, inverse, keep = pair_waves(pair, cut_ref)
 
+        spot = lax.broadcasted_iota(jnp.int32, (DEPTH, 128), 1)
+
         def of_pair(a, c):
-            halves = []
+            found = []
             for odd in range(2):
                 re, im = (
                     spectra[odd, 128 * a + 64 * k : 128 * a + 64 * (k + 1), :] for k in range(2)
@@ -536,15 +558,19 @@
                 last = spectra[odd, 384:392, :]
                 for x in range(1, BAND):
                     last = last + spectra[odd, 384 + 8 * x : 392 + 8 * x, :]
-                re64, im64 = last[2 * a : 2 * a + 1], last[2 * a + 1 : 2 * a + 2]
+                zeros = jnp.zeros((7, 256), f32)
+                re = jnp.concatenate([re, last[2 * a : 2 * a + 1], zeros], axis=0)
+                im = jnp.concatenate([im, last[2 * a + 1 : 2 * a + 2], zeros], axis=0)
                 if c == 0:
-                    value, value64 = (r[:, :256] + i[:, 256:] for r, i in ((re, im), (re64, im64)))
+                    one, other = re[:, :128], im[:, 128:]
                 else:
-                    value, value64 = (i[:, :256] - r[:, 256:] for r, i in ((re, im), (re64, im64)))
-                value = jnp.concatenate([value, value64, jnp.zeros((7, 256), f32)], axis=0)
-                halves.append(pltpu.roll(value, 64, 1) if odd else value)
-            even, odd = halves
-            return jnp.concatenate([even[:, :128], even[:, 128:] + odd[:, :128], odd[:, 128:]], axis=1)
+                    one, other = im[:, :128], -re[:, 128:]
+                found.append((one + other, jnp.where(spot == 64, one - other, one + other)))
+            (even, even_low), (odd, odd_low) = found
+            even_low, odd = pltpu.roll(even_low, 64, 1), pltpu.roll(odd, 64, 1)
+            return jnp.concatenate(
+                [even, jnp.where(spot < 64, even_low, odd), jnp.where(spot < 64, odd, odd_low)], axis=1
+            )
 
         for c in range(2):
             old = project([old_ref[c, a, :, :] for a in range(3)], waves, inverse, keep)
@@ -581,10 +607,10 @@
         out_specs=(ANY, ANY, ANY),
         scratch_shapes=[
             pltpu.VMEM((3, 2, 3, DEPTH, 384), f32),
-            pltpu.VMEM((2, 512, 512), bf16),
+            pltpu.VMEM((2, 512, 256), bf16),
             *(pltpu.VMEM(t.shape, bf16) for t in (ey, zt, zb, eyt)),
-            pltpu.VMEM((2304, 512), f32),
-            pltpu.VMEM((40, 512), f32),
+            pltpu.VMEM((2, 2304, 256), f32),
+            pltpu.VMEM((2, 40, 256), f32),
             pltpu.VMEM((4, 40, 128), f32),
             pltpu.VMEM((3, BAND * STRIDE, 128), f32),
             pltpu.VMEM((PARTS, SLOTS, 8, 128), f32),
@@ -617,7 +643,7 @@
         out_shape=(shape((2, 3, 96, 1152), f32), shape((1,), f32), shape((1,), f32)),
         in_specs=[SM, SM, SM, block, whole(chunks), whole(last), whole(stats), whole(cs)],
         out_specs=(pl.BlockSpec((2, 3, 96, 384), lambda i: (0, 0, 0, i)), SM, SM),
-        scratch_shapes=[pltpu.VMEM((432, GRID), f32), pltpu.VMEM((2, 432, 512), f32)],
+        scratch_shapes=[pltpu.VMEM((432, GRID), f32), pltpu.VMEM((2, 432, 256), f32)],
         compiler_params=pltpu.CompilerParams(vmem_limit_bytes=VMEM_BYTES),
     )(cutoffs, time_step, power, velocity_hat, chunks, last, stats, cs)
 

time: 79.3 us -> 76.6 us (0.966)
  Pallas kernels: 77.2 us -> 74.5 us
    pallas_call x1, Pallas kernels: 69.4 us -> 67.5 us  [on_device(): pl.pallas_call(exchange_kernel, out_shape=(shape((3, BAND, PARTS, 8, 128)...]
    pallas_call x1, Pallas kernels: 7.83 us -> 6.93 us  [on_device(): pl.pallas_call(close_kernel, grid=(3,), out_shape=(shape((2, 3, 96, 1152)...]
where the time goes in v5:
time: 76.6 us; the launch traced here: 76.4 us
  Pallas kernels  74.5 us (97%)
  between operations  1.93 us (3%)
    pallas_call x1, Pallas kernels, on_device(): pl.pallas_call(exchange_kernel, out_shape=(shape((3, BAND, PARTS, 8, 128)...  67.5 us
    pallas_call x1, Pallas kernels, on_device(): pl.pallas_call(close_kernel, grid=(3,), out_shape=(shape((2, 3, 96, 1152)...  6.93 us

profile of v5, /device:TPU:0, one launch (start us, length us, event | category | flops | bytes accessed | tf_op | source)
XLA Modules:
  0.0 76.4 jit_solution(17629257833883966187)
XLA Ops:
  1.9 67.5 %shard_map.121 = (f32[3,6,32,8,128]{4,3,2,1,0:T(8,128)}, f32[32,8,128]{2,1,0:T(8,128)}, f32[32,8,128]{2,1,0:T(8,128)}) custom-call(s32[3]{0:T(128)} %cut_ref.3, f32[2,3,96,1152]{3,2,1,0:T(8,128)} %old_ref.1, bf16[2,256,384]{2,1,0:T(8,128)(2,1)} %constant.12.clone.tx_hbm, bf16[2,384,256]{2,1,0:T(8,128)(2,1)} %constant.14.clone.ey_hbm, ...), custom_call_target="tpu_custom_call" | custom-call | tf_op jit(solution)/shard_map/pallas_call | solution.py:599
  69.5 6.9 %shard_map.122 = (f32[2,3,96,1152]{3,2,1,0:T(8,128)}, f32[1]{0:T(128)}, f32[1]{0:T(128)}) custom-call(s32[3]{0:T(128)} %cut_ref.3, f32[1]{0:T(128)S(6)} %copy.13.dt_ref, f32[1]{0:T(128)S(6)} %copy.14.power_ref, f32[2,3,96,1152]{3,2,1,0:T(8,128)} %old_ref.1, f32[3,1536,128]{2,1,0:T(8,128)} %bitcast.2, f32[256,128]{1,0:T(8,128)} %bitcast.3, ...), custom_call_target="tpu_custom_call" | custom-call | tf_op jit(solution)/shard_map/pallas_call | solution.py:640

commit v6 on v5

--- a/solution.py
+++ b/solution.py
@@ -311,8 +311,8 @@
         for j, offset in others:
             device = peer(offset)
             remote(
-                ready.at[flat(device), 0],
-                arrived.at[0, me],
+                ready.at[flat(device), 0, pl.ds(0, BAND), :],
+                arrived.at[0, me, pl.ds(0, BAND), :],
                 send_sems.at[1],
                 recv_sems.at[BAND],
                 device,
@@ -381,7 +381,7 @@
         pl.when(jnp.logical_not(live))(lambda: await_count(len(LIVE)))
 
     def await_last(count):
-        part = arrived.at[0, pl.ds(0, count)]
+        part = arrived.at[0, pl.ds(0, count), pl.ds(0, BAND), :]
         remote(part, part, send_sems.at[1], recv_sems.at[BAND], (px, pz)).wait_recv()
 
     from_live(await_last)
@@ -447,7 +447,7 @@
     back64[GRID:] = jnp.where(lane % 2 == 0, pltpu.roll(q, 127, 1), -pltpu.roll(q, 1, 1))
     wide = table_by_data(eyt_ref, back64[...], ((1,), (0,)))
     closed64[...] = wide.reshape(len(LIVE), 8, 128)
-    stat[...] = jnp.where(lane8 == 0, jnp.max(top[...]), jnp.sum(total[...]))
+    stat[...] = jnp.where(lane8[:1] == 0, jnp.max(top[...]), jnp.sum(total[...]))
 
     def stat_copy(device):
         return remote(stat, stats_hbm.at[me], back_sems.at[2], back_sems.at[3], device)
@@ -459,8 +459,8 @@
         @pl.when(is_live(flat(device)))
         def _():
             remote(
-                closed64.at[place(flat(device))],
-                last_hbm.at[me],
+                closed64.at[place(flat(device)), pl.ds(0, BAND), :],
+                last_hbm.at[me, pl.ds(0, BAND), :],
                 back_sems.at[4],
                 back_sems.at[5],
                 device,
@@ -496,18 +496,18 @@
 
     def await_sent(count):
         sent(closed.at[:, :, pl.ds(0, count), pl.ds(0, BAND), :], back_sems.at[0])
-        sent(closed64.at[pl.ds(0, count)], back_sems.at[4])
+        sent(closed64.at[pl.ds(0, count), pl.ds(0, BAND), :], back_sems.at[4])
 
     from_live(await_sent)
-    sent(arrived.at[0, rest], back_sems.at[2])
+    sent(arrived.at[0, rest, pl.ds(0, 1), :], back_sems.at[2])
     came(stats_hbm.at[rest], back_sems.at[3])
 
     @pl.when(live)
     def _():
         sent(ready.at[rest, pl.ds(1, SLOTS - 1), pl.ds(0, BAND), :], send_sems.at[0])
-        sent(ready.at[rest, 0], send_sems.at[1])
+        sent(ready.at[rest, 0, pl.ds(0, BAND), :], send_sems.at[1])
         came(out_hbm.at[:, :, rest, pl.ds(0, BAND), :], back_sems.at[1])
-        came(last_hbm.at[rest], back_sems.at[5])
+        came(last_hbm.at[rest, pl.ds(0, BAND), :], back_sems.at[5])
 
 
 def close_kernel(
@@ -601,7 +601,7 @@
         out_shape=(
             shape((3, BAND, PARTS, 8, 128), f32),
             shape((PARTS, 8, 128), f32),
-            shape((PARTS, 8, 128), f32),
+            shape((PARTS, 1, 128), f32),
         ),
         in_specs=[SM] + [ANY] * 6,
         out_specs=(ANY, ANY, ANY),
@@ -624,7 +624,7 @@
             pltpu.VMEM((len(LIVE), 8, 128), f32),
             pltpu.VMEM((8, GRID), f32),
             pltpu.VMEM((8, GRID), f32),
-            pltpu.VMEM((8, 128), f32),
+            pltpu.VMEM((1, 128), f32),
             dma((11,)),
             dma((2,)),
             dma((BAND + 1,)),

time: 76.6 us -> 75 us (0.979)
  Pallas kernels: 74.5 us -> 72.9 us
    pallas_call x1, Pallas kernels: 67.5 us -> 66.1 us  [on_device(): pl.pallas_call(exchange_kernel, out_shape=(shape((3, BAND, PARTS, 8, 128)...]
where the time goes in v6:
time: 75 us; the launch traced here: 74.9 us
  Pallas kernels  72.9 us (97%)
  between operations  1.93 us (3%)
    pallas_call x1, Pallas kernels, on_device(): pl.pallas_call(exchange_kernel, out_shape=(shape((3, BAND, PARTS, 8, 128)...  66.1 us
    pallas_call x1, Pallas kernels, on_device(): pl.pallas_call(close_kernel, grid=(3,), out_shape=(shape((2, 3, 96, 1152)...  6.87 us

profile of v6, /device:TPU:0, one launch (start us, length us, event | category | flops | bytes accessed | tf_op | source)
XLA Modules:
  0.0 74.9 jit_solution(8551132736260523034)
XLA Ops:
  1.9 66.1 %shard_map.121 = (f32[3,6,32,8,128]{4,3,2,1,0:T(8,128)}, f32[32,8,128]{2,1,0:T(8,128)}, f32[32,1,128]{2,1,0:T(1,128)}) custom-call(s32[3]{0:T(128)} %cut_ref.3, f32[2,3,96,1152]{3,2,1,0:T(8,128)} %old_ref.1, bf16[2,256,384]{2,1,0:T(8,128)(2,1)} %constant.12.clone.tx_hbm, bf16[2,384,256]{2,1,0:T(8,128)(2,1)} %constant.14.clone.ey_hbm, ...), custom_call_target="tpu_custom_call" | custom-call | tf_op jit(solution)/shard_map/pallas_call | solution.py:599
  68.0 6.9 %shard_map.122 = (f32[2,3,96,1152]{3,2,1,0:T(8,128)}, f32[1]{0:T(128)}, f32[1]{0:T(128)}) custom-call(s32[3]{0:T(128)} %cut_ref.3, f32[1]{0:T(128)S(6)} %copy.13.dt_ref, f32[1]{0:T(128)S(6)} %copy.14.power_ref, f32[2,3,96,1152]{3,2,1,0:T(8,128)} %old_ref.1, f32[3,1536,128]{2,1,0:T(8,128)} %bitcast.2, f32[256,128]{1,0:T(8,128)} %bitcast.3, ...), custom_call_target="tpu_custom_call" | custom-call | tf_op jit(solution)/shard_map/pallas_call | solution.py:640

commit v7 on v6

--- a/solution.py
+++ b/solution.py
@@ -124,6 +124,7 @@
 
 SLOTS = 31
 STRIDE = 520
+AHEAD = 3
 
 
 def slot_of(f, x):
@@ -304,6 +305,35 @@
                         at = (2 * pair + odd) * STRIDE + 256 * c
                         made[group, at : at + 256, :] = wide[:, 128 * odd : 128 * (odd + 1)]
 
+    def spread(x, carry):
+        def fill(d, write):
+            for group in range(3):
+                re, im = (
+                    made[group, pl.ds(256 * c + 8 * d + x, BAND, stride=STRIDE), :]
+                    for c in range(2)
+                )
+                if group == 2:
+                    write(4, jnp.where(low6, re, im))
+                else:
+                    write(2 * group, jnp.where(low6, re, pltpu.roll(im, 64, 1)))
+                    write(2 * group + 1, jnp.where(low6, pltpu.roll(re, 64, 1), im))
+
+        for j, offset in others:
+            device = peer(offset)
+            d = flat(device)
+
+            def write(f, value):
+                ready[d, slot_of(f, x), :BAND, :] = value
+
+            fill(d, write)
+            first_copy(x, device).start()
+
+        def keep_own(f, value):
+            arrived[slot_of(f, x), me, :BAND, :] = value
+
+        fill(me, keep_own)
+        return carry
+
     pl.semaphore_wait(barrier, PARTS - 1)
 
     @pl.when(live)
@@ -319,36 +349,7 @@
             ).start()
         arrived[0, me] = ready[me, 0]
 
-        def spread(x, carry):
-            def fill(d, write):
-                for group in range(3):
-                    re, im = (
-                        made[group, pl.ds(256 * c + 8 * d + x, BAND, stride=STRIDE), :]
-                        for c in range(2)
-                    )
-                    if group == 2:
-                        write(4, jnp.where(low6, re, im))
-                    else:
-                        write(2 * group, jnp.where(low6, re, pltpu.roll(im, 64, 1)))
-                        write(2 * group + 1, jnp.where(low6, pltpu.roll(re, 64, 1), im))
-
-            for j, offset in others:
-                device = peer(offset)
-                d = flat(device)
-
-                def write(f, value):
-                    ready[d, slot_of(f, x), :BAND, :] = value
-
-                fill(d, write)
-                first_copy(x, device).start()
-
-            def keep_own(f, value):
-                arrived[slot_of(f, x), me, :BAND, :] = value
-
-            fill(me, keep_own)
-            return carry
-
-        lax.fori_loop(0, BAND, spread, 0)
+        lax.fori_loop(0, AHEAD, spread, 0)
 
     top[...] = jnp.zeros_like(top)
     total[...] = jnp.zeros_like(total)
@@ -401,6 +402,7 @@
             remote(part, part, send_sems.at[0], recv_sems.at[x], (px, pz)).wait_recv()
 
         from_live(await_plane)
+        pl.when(live & (x + AHEAD < BAND))(lambda: spread(x + AHEAD, None))
         tiles = [arrived[slot_of(f, x)].reshape(256, 128) for f in range(2)]
         to_grid(x, 0, tiles)
         turned = sign * pltpu.roll(ky * tiles[1] - kz * tiles[0], 64, 1)
@@ -443,18 +445,21 @@
 
     lax.fori_loop(0, BAND, plane, 0)
 
+    stat[...] = jnp.where(lane8[:1] == 0, jnp.max(top[...]), jnp.sum(total[...]))
+
+    def stat_copy(device):
+        return remote(stat, stats_hbm.at[me], back_sems.at[2], back_sems.at[3], device)
+
+    for _, offset in others:
+        stat_copy(peer(offset)).start()
+
     q = back64[:GRID]
     back64[GRID:] = jnp.where(lane % 2 == 0, pltpu.roll(q, 127, 1), -pltpu.roll(q, 1, 1))
     wide = table_by_data(eyt_ref, back64[...], ((1,), (0,)))
     closed64[...] = wide.reshape(len(LIVE), 8, 128)
-    stat[...] = jnp.where(lane8[:1] == 0, jnp.max(top[...]), jnp.sum(total[...]))
-
-    def stat_copy(device):
-        return remote(stat, stats_hbm.at[me], back_sems.at[2], back_sems.at[3], device)
 
     for j, offset in others:
         device = peer(offset)
-        stat_copy(device).start()
 
         @pl.when(is_live(flat(device)))
         def _():

time: 75 us -> 75.1 us (level)
  no operation moved by 1% of the time
where the time goes in v7:
time: 75.1 us; the launch traced here: 74.9 us
  Pallas kernels  73 us (97%)
  between operations  1.93 us (3%)
    pallas_call x1, Pallas kernels, on_device(): pl.pallas_call(exchange_kernel, out_shape=(shape((3, BAND, PARTS, 8, 128)...  66.1 us
    pallas_call x1, Pallas kernels, on_device(): pl.pallas_call(close_kernel, grid=(3,), out_shape=(shape((2, 3, 96, 1152)...  6.87 us

profile of v7, /device:TPU:0, one launch (start us, length us, event | category | flops | bytes accessed | tf_op | source)
XLA Modules:
  0.0 74.9 jit_solution(7680738157307128800)
XLA Ops:
  1.9 66.1 %shard_map.121 = (f32[3,6,32,8,128]{4,3,2,1,0:T(8,128)}, f32[32,8,128]{2,1,0:T(8,128)}, f32[32,1,128]{2,1,0:T(1,128)}) custom-call(s32[3]{0:T(128)} %cut_ref.3, f32[2,3,96,1152]{3,2,1,0:T(8,128)} %old_ref.1, bf16[2,256,384]{2,1,0:T(8,128)(2,1)} %constant.12.clone.tx_hbm, bf16[2,384,256]{2,1,0:T(8,128)(2,1)} %constant.14.clone.ey_hbm, ...), custom_call_target="tpu_custom_call" | custom-call | tf_op jit(solution)/shard_map/pallas_call | solution.py:604
  68.0 6.9 %shard_map.122 = (f32[2,3,96,1152]{3,2,1,0:T(8,128)}, f32[1]{0:T(128)}, f32[1]{0:T(128)}) custom-call(s32[3]{0:T(128)} %cut_ref.3, f32[1]{0:T(128)S(6)} %copy.13.dt_ref, f32[1]{0:T(128)S(6)} %copy.14.power_ref, f32[2,3,96,1152]{3,2,1,0:T(8,128)} %old_ref.1, f32[3,1536,128]{2,1,0:T(8,128)} %bitcast.2, f32[256,128]{1,0:T(8,128)} %bitcast.3, ...), custom_call_target="tpu_custom_call" | custom-call | tf_op jit(solution)/shard_map/pallas_call | solution.py:645
